TPU v7x, 128 devices: a whole 4x4x4 slice. The times are simulated.
128 devices in a mesh: seg: 32 (over y, z, core), grp: 4 (over x).
Axes of the slice: x: 4, y: 4, z: 4, core: 2. Of those that a mesh axis runs over, the one named last changes fastest.
Arguments:
- basis: float32 [8, 3072, 128], P(None, ('seg', 'grp')), may hold values from -6 to 6
- coords: float32 [3072, 3, 128], P(('seg', 'grp')), may hold values from 0 to 4
- areas: float32 [3072, 128], P(('seg', 'grp')), may hold values from 0.5 to 2
- p2m: bfloat16 [3072, 121, 128], P(('seg', 'grp')), may hold values from -0.5 to 0.5
- l2p: bfloat16 [3072, 128, 121], P(('seg', 'grp')), may hold values from -0.5 to 0.5
- m2l: bfloat16 [316, 121, 121], replicated, may hold values from -0.0390625 to 0.0390625
- counts: int32 [128], P(('seg', 'grp')), may hold values from 8 to 24
- near_list: int32 [3072, 27], P(('seg', 'grp')), may hold values from 0 to 287
- far_list: int32 [3072, 189], P(('seg', 'grp')), may hold values from 0 to 287
- far_offset: int32 [3072, 189], P(('seg', 'grp')), may hold values from 0 to 315
Outputs:
- new_vector: float32 [3072, 128], P(('seg', 'grp'))
- hessenberg: float32 [9], replicated
Inputs may be any that keep to these rules, and one draw needn't show every extreme that they name: `near_list`: window indices follow the rule of the steps; entries may name empty slots or leaves beyond the ends of the curve, which contribute nothing. A device's live leaves are its first counts slots.
All inputs are finite; a program needn't handle non-finite values.
Results may differ from a plain program's by a relative error of at most 0.0012.
Values sent between devices are 32-bit elements; how exact they have to be, the bound alone decides.
A program may use at most 64 MiB of HBM per device.

v0:
```python
import math

import jax
import jax.numpy as jnp
from jax import lax
from jax.sharding import Mesh
from jax.sharding import PartitionSpec as P

SEG = ("seg_0", "seg_1", "seg_2")
SEG_GRP = ("seg_0", "seg_1", "seg_2", "grp")


four_pi = 12.566370614359172
epsilon = 1e-06
highest = lax.Precision.HIGHEST


def from_everyone(value, axis):
    copies = jnp.broadcast_to(value, (lax.axis_size(axis), *value.shape))
    return lax.all_to_all(copies, axis, split_axis=0, concat_axis=0, tiled=True)


def in_order(pieces, dim):
    lengths = list(pieces.shape[1:])
    lengths[dim] *= pieces.shape[0]
    return jnp.moveaxis(pieces, 0, dim).reshape(lengths)


def gathered_copies(value, axis, dim):
    pieces = from_everyone(value, axis)
    return in_order(pieces, dim)


def in_one_piece(arrays, axis, dim, along):
    widths = [math.prod(a.shape[along:]) for a in arrays]
    both = jnp.concatenate(
        [a.reshape(*a.shape[:along], w) for a, w in zip(arrays, widths)], axis=along
    )
    whole = gathered_copies(both, axis, dim)
    pieces = jnp.split(whole, [sum(widths[:k]) for k in range(1, len(widths))], axis=along)
    return tuple(
        (b.reshape(*whole.shape[:along], *a.shape[along:]) for a, b in zip(arrays, pieces))
    )


def with_halo(cells, sides, width):
    for axis, dim in sides:
        count = lax.axis_size(axis)
        ends = count - 1
        head = lax.slice_in_dim(cells, 0, width, axis=dim)
        tail = lax.slice_in_dim(cells, cells.shape[dim] - width, cells.shape[dim], axis=dim)
        cells = jnp.concatenate(
            [
                lax.ppermute(tail, axis, [(i, (i + 1) % count) for i in range(ends)]),
                cells,
                lax.ppermute(head, axis, [((i + 1) % count, i) for i in range(ends)]),
            ],
            axis=dim,
        )
    return cells


def by_axis(value, axes):
    for axis in axes:
        value = lax.psum(value, axis)
    return value


def near_field(coords, wide_panels, near_list):
    leaf_count = coords.shape[0]
    panels = coords.shape[2]

    def near_step(running, column):
        source = jnp.take(wide_panels, column, axis=0)
        square = jnp.zeros((leaf_count, panels, panels), jnp.float32)
        for component in range(3):
            spread = coords[:, component, :, None] - source[:, component, None, :]
            square = square + spread * spread
        source_area = source[:, 3, None, :]
        kernel = source_area / (four_pi * jnp.sqrt(square + source_area))
        return (running + jnp.sum(kernel * source[:, 4, None, :], axis=2), None)

    result, _ = lax.scan(near_step, jnp.zeros((leaf_count, panels), jnp.float32), near_list.T)
    return result


def far_field(wide_poles, m2l, far_list, far_offset):
    offsets = m2l.shape[0]
    gathered = jnp.take(wide_poles, far_list, axis=0)
    offset_hot = (
        far_offset[:, :, None] == lax.broadcasted_iota(jnp.int32, (1, 1, offsets), 2)
    ).astype(jnp.float32)
    summed = jnp.einsum("tfo,tfk->tok", offset_hot, gathered, precision=highest)
    return jnp.einsum("tok,oik->ti", summed, m2l.astype(jnp.float32), precision=highest)


def on_device(basis, coords, areas, p2m, l2p, m2l, counts, near_list, far_list, far_offset):
    leaf_count, panels = areas.shape
    krylov = basis.shape[0]
    slots = lax.broadcasted_iota(jnp.int32, (leaf_count, 1), 0)
    live_mask = (slots < counts[0]).astype(jnp.float32)
    current = basis[krylov - 1] * live_mask
    rounded = current.astype(jnp.bfloat16)
    multipoles = jnp.einsum("lkp,lp->lk", p2m, rounded, preferred_element_type=jnp.float32)
    packed = jnp.concatenate([coords, areas[:, None, :], current[:, None, :]], axis=1)
    group_panels, group_poles = in_one_piece((packed, multipoles), "grp", 0, 1)
    wide_panels, wide_poles = (
        with_halo(group_panels, ((SEG, 0),), group_panels.shape[0]),
        with_halo(group_poles, ((SEG, 0),), group_panels.shape[0]),
    )
    nearby = near_field(coords, wide_panels, near_list)
    local = far_field(wide_poles, m2l, far_list, far_offset).astype(jnp.bfloat16)
    distant = jnp.einsum("lpk,lk->lp", l2p, local, preferred_element_type=jnp.float32)
    image = (0.5 * current + nearby + distant) * live_mask
    masked = basis * live_mask[None]
    products = jnp.einsum("jlp,lp->j", masked, image, precision=highest)
    live_panels = jnp.sum(live_mask) * panels
    gram = jnp.einsum("ilp,jlp->ij", masked, masked, precision=highest)
    summed, population, gram_sum, energy = (
        by_axis(products, SEG_GRP),
        by_axis(live_panels, SEG_GRP),
        by_axis(gram, SEG_GRP),
        by_axis(jnp.sum(image * image), SEG_GRP),
    )
    coefficients = summed / population
    residue = image - jnp.einsum("j,jlp->lp", coefficients, masked, precision=highest)
    curvature = jnp.dot(
        coefficients, jnp.dot(gram_sum, coefficients, precision=highest), precision=highest
    )
    squares = energy - 2.0 * jnp.dot(coefficients, summed, precision=highest) + curvature
    scale = jnp.sqrt(squares / population + epsilon)
    return (residue / scale, jnp.concatenate([coefficients, scale[None]]))


def solution(mesh):
    torus = Mesh(
        mesh.devices.reshape(4, 4, 2, mesh.shape["grp"]), ("seg_0", "seg_1", "seg_2", "grp")
    )
    in_specs = (
        P(None, SEG_GRP, None),
        P(SEG_GRP, None, None),
        P(SEG_GRP, None),
        P(SEG_GRP, None, None),
        P(SEG_GRP, None, None),
        P(),
        P(SEG_GRP),
        P(SEG_GRP, None),
        P(SEG_GRP, None),
        P(SEG_GRP, None),
    )
    out_specs = (P(SEG_GRP, None), P())
    return jax.shard_map(
        on_device, mesh=torus, in_specs=in_specs, out_specs=out_specs, check_vma=False
    )
```

profile of v0, /device:TPU:1, one launch (start us, length us, event | category | flops | bytes accessed | tf_op | source)
XLA Modules:
  0.0 193.8 jit_solution(17818676448152926383)
XLA Ops:
  6.1 4.8 %all-to-all-start = ((f32[4,24,761]{2,1,0:T(8,128)}), f32[4,24,761]{2,1,0:T(8,128)S(1)}, u32[]{:S(2)}, u32[]{:S(2)}) async-start(f32[4,24,761]{2,1,0:T(8,128)} %broadcast_in_dim.39), calls=%async_computation | async-start | bytes 589824 | tf_op jit(solution)/shard_map/all_to_all | solution.py:20
  11.5 5.3 %all-to-all-done = f32[4,24,761]{2,1,0:T(8,128)S(1)} async-done(((f32[4,24,761]{2,1,0:T(8,128)}), f32[4,24,761]{2,1,0:T(8,128)S(1)}, u32[]{:S(2)}, u32[]{:S(2)}) %all-to-all-start) | async-done | bytes 292256 | tf_op jit(solution)/shard_map/all_to_all | solution.py:20
  16.8 4.0 %collective-permute-start.3 = (f32[96,121]{1,0:T(8,128)S(1)}, f32[96,121]{1,0:T(8,128)S(1)}, u32[]{:S(2)}, u32[]{:S(2)}) collective-permute-start(f32[96,121]{1,0:T(8,128)S(1)} %split.9), channel_id=1, source_target_pairs={{4,0},{8,4},{12,8},{16,12},{20,16},{24,20},{28,24},{32,28},{36,32}... | collective-permute-start | bytes 139400 | tf_op jit(solution)/shard_map/ppermute | solution.py:56
  20.8 3.4 %collective-permute-start.2 = (f32[96,121]{1,0:T(8,128)S(1)}, f32[96,121]{1,0:T(8,128)S(1)}, u32[]{:S(2)}, u32[]{:S(2)}) collective-permute-start(f32[96,121]{1,0:T(8,128)S(1)} %split.9), channel_id=1, source_target_pairs={{0,4},{4,8},{8,12},{12,16},{16,20},{20,24},{24,28},{28,32},{32,36}... | collective-permute-start | bytes 139400 | tf_op jit(solution)/shard_map/ppermute | solution.py:54
  28.6 3.6 %collective-permute-start = (f32[96,5,128]{0,2,1:T(8,128)}, f32[96,5,128]{0,2,1:T(8,128)}, u32[]{:S(2)}, u32[]{:S(2)}) collective-permute-start(f32[96,5,128]{0,2,1:T(8,128)} %bitcast.9), channel_id=1, source_target_pairs={{0,4},{4,8},{8,12},{12,16},{16,20},{20,24},{24,28},{28,32},{32,36}... | collective-permute-start | bytes 737288 | tf_op jit(solution)/shard_map/ppermute | solution.py:54
  32.3 7.4 %gather_fusion.1 = f32[4536,121]{1,0:T(8,128)S(1)} fusion(f32[288,121]{1,0:T(8,128)S(1)} %pad_maximum_fusion.1, s32[5120]{0:T(1024)S(1)} %pad_clamp_fusion.1), kind=kCustom, calls=%fused_computation.1 | custom fusion | bytes 4408992 | tf_op jit(solution)/shard_map/jit(_take)/gather | solution.py:89
  41.3 10.6 %fusion.3 = f32[24,316,121]{2,1,0:T(8,128)S(1)} fusion(s32[24,189]{1,0:T(8,128)S(1)} %copy-done.4, f32[24,189,121]{2,1,0:T(8,128)} %reshape.114, pred[24,189]{1,0:T(8,128)(4,1)S(1)} %compare_and_fusion.1), kind=kOutput, calls=%fused_computation.17 | convolution fusion | flops 2083244160 | bytes 5888760 | tf_op jit(solution)/shard_map/tfo,tfk->tok/dot_general | solution.py:93
  52.0 16.4 %fusion.19 = bf16[24,121,1]{1,0,2:T(8,128)(2,1)S(1)} fusion(bf16[316,121,121]{2,0,1:T(8,128)(2,1)} %param.17, f32[24,316,121]{2,1,0:T(8,128)S(1)} %fusion.3), kind=kOutput, calls=%fused_computation.25 | convolution fusion | flops 1332450944 | bytes 12929576 | tf_op jit(solution)/shard_map/tok,oik->ti/dot_general | solution.py:94
  70.9 82.7 %while.11 = (s32[]{:T(128)}, f32[24,128]{1,0:T(8,128)S(1)}, s32[27,24]{1,0:T(8,128)S(1)}, f32[288,5,128]{2,1,0:T(8,128)S(1)}, f32[24,3,128]{2,0,1:T(8,128)S(1)}, /*index=5*/s32[]{:T(128)}, s32[]{:T(128)}) while((s32[]{:T(128)}, f32[24,128]{1,0:T(8,128)S(1)}, s32[27,24]{1,0:T(8,128)S(1)}, f32[288,5,128]{2,1,0:T(8,128)S(1)}, ...), condition=%wide.region_2.3_spmd.clone, body=%wide.region_0.2_spmd.clone.sunk | while | flops 5131483 | bytes 594551 | solution.py:83
  71.7 2.2 %multiply_reduce_fusion.4 = f32[24,128]{1,0:T(8,128)S(1)} fusion(f32[24,128]{1,0:T(8,128)S(1)} %bitcast.99, f32[24,128]{1,0:T(8,128)S(1)} %bitcast.100, f32[24,128]{1,0:T(8,128)S(1)} %get-tuple-element.137, f32[24,128]{1,0:T(8,128)S(1)} %bitcast.101, f32[24,128]{1,0:T(8,128)S(1)} %get-tuple-element.139, f32[24,128]{1,0:T(8,128)S(1)} %bitcast.102, ...), kind=kLoop, calls=%fused_computation.2.clone.1 | loop fusion | flops 5108736 | bytes 110592 | tf_op jit(solution)/shard_map/while/body/eval_jaxpr/reduce_sum | solution.py:81
  74.8 2.2 %multiply_reduce_fusion.4 = f32[24,128]{1,0:T(8,128)S(1)} fusion(f32[24,128]{1,0:T(8,128)S(1)} %bitcast.99, f32[24,128]{1,0:T(8,128)S(1)} %bitcast.100, f32[24,128]{1,0:T(8,128)S(1)} %get-tuple-element.137, f32[24,128]{1,0:T(8,128)S(1)} %bitcast.101, f32[24,128]{1,0:T(8,128)S(1)} %get-tuple-element.139, f32[24,128]{1,0:T(8,128)S(1)} %bitcast.102, ...), kind=kLoop, calls=%fused_computation.2.clone.1 | loop fusion | flops 5108736 | bytes 110592 | tf_op jit(solution)/shard_map/while/body/eval_jaxpr/reduce_sum | solution.py:81
  77.8 2.2 %multiply_reduce_fusion.4 = f32[24,128]{1,0:T(8,128)S(1)} fusion(f32[24,128]{1,0:T(8,128)S(1)} %bitcast.99, f32[24,128]{1,0:T(8,128)S(1)} %bitcast.100, f32[24,128]{1,0:T(8,128)S(1)} %get-tuple-element.137, f32[24,128]{1,0:T(8,128)S(1)} %bitcast.101, f32[24,128]{1,0:T(8,128)S(1)} %get-tuple-element.139, f32[24,128]{1,0:T(8,128)S(1)} %bitcast.102, ...), kind=kLoop, calls=%fused_computation.2.clone.1 | loop fusion | flops 5108736 | bytes 110592 | tf_op jit(solution)/shard_map/while/body/eval_jaxpr/reduce_sum | solution.py:81
  80.9 2.2 %multiply_reduce_fusion.4 = f32[24,128]{1,0:T(8,128)S(1)} fusion(f32[24,128]{1,0:T(8,128)S(1)} %bitcast.99, f32[24,128]{1,0:T(8,128)S(1)} %bitcast.100, f32[24,128]{1,0:T(8,128)S(1)} %get-tuple-element.137, f32[24,128]{1,0:T(8,128)S(1)} %bitcast.101, f32[24,128]{1,0:T(8,128)S(1)} %get-tuple-element.139, f32[24,128]{1,0:T(8,128)S(1)} %bitcast.102, ...), kind=kLoop, calls=%fused_computation.2.clone.1 | loop fusion | flops 5108736 | bytes 110592 | tf_op jit(solution)/shard_map/while/body/eval_jaxpr/reduce_sum | solution.py:81
  84.0 2.2 %multiply_reduce_fusion.4 = f32[24,128]{1,0:T(8,128)S(1)} fusion(f32[24,128]{1,0:T(8,128)S(1)} %bitcast.99, f32[24,128]{1,0:T(8,128)S(1)} %bitcast.100, f32[24,128]{1,0:T(8,128)S(1)} %get-tuple-element.137, f32[24,128]{1,0:T(8,128)S(1)} %bitcast.101, f32[24,128]{1,0:T(8,128)S(1)} %get-tuple-element.139, f32[24,128]{1,0:T(8,128)S(1)} %bitcast.102, ...), kind=kLoop, calls=%fused_computation.2.clone.1 | loop fusion | flops 5108736 | bytes 110592 | tf_op jit(solution)/shard_map/while/body/eval_jaxpr/reduce_sum | solution.py:81
  87.0 2.2 %multiply_reduce_fusion.4 = f32[24,128]{1,0:T(8,128)S(1)} fusion(f32[24,128]{1,0:T(8,128)S(1)} %bitcast.99, f32[24,128]{1,0:T(8,128)S(1)} %bitcast.100, f32[24,128]{1,0:T(8,128)S(1)} %get-tuple-element.137, f32[24,128]{1,0:T(8,128)S(1)} %bitcast.101, f32[24,128]{1,0:T(8,128)S(1)} %get-tuple-element.139, f32[24,128]{1,0:T(8,128)S(1)} %bitcast.102, ...), kind=kLoop, calls=%fused_computation.2.clone.1 | loop fusion | flops 5108736 | bytes 110592 | tf_op jit(solution)/shard_map/while/body/eval_jaxpr/reduce_sum | solution.py:81
  90.1 2.2 %multiply_reduce_fusion.4 = f32[24,128]{1,0:T(8,128)S(1)} fusion(f32[24,128]{1,0:T(8,128)S(1)} %bitcast.99, f32[24,128]{1,0:T(8,128)S(1)} %bitcast.100, f32[24,128]{1,0:T(8,128)S(1)} %get-tuple-element.137, f32[24,128]{1,0:T(8,128)S(1)} %bitcast.101, f32[24,128]{1,0:T(8,128)S(1)} %get-tuple-element.139, f32[24,128]{1,0:T(8,128)S(1)} %bitcast.102, ...), kind=kLoop, calls=%fused_computation.2.clone.1 | loop fusion | flops 5108736 | bytes 110592 | tf_op jit(solution)/shard_map/while/body/eval_jaxpr/reduce_sum | solution.py:81
  93.2 2.2 %multiply_reduce_fusion.4 = f32[24,128]{1,0:T(8,128)S(1)} fusion(f32[24,128]{1,0:T(8,128)S(1)} %bitcast.99, f32[24,128]{1,0:T(8,128)S(1)} %bitcast.100, f32[24,128]{1,0:T(8,128)S(1)} %get-tuple-element.137, f32[24,128]{1,0:T(8,128)S(1)} %bitcast.101, f32[24,128]{1,0:T(8,128)S(1)} %get-tuple-element.139, f32[24,128]{1,0:T(8,128)S(1)} %bitcast.102, ...), kind=kLoop, calls=%fused_computation.2.clone.1 | loop fusion | flops 5108736 | bytes 110592 | tf_op jit(solution)/shard_map/while/body/eval_jaxpr/reduce_sum | solution.py:81
  96.2 2.2 %multiply_reduce_fusion.4 = f32[24,128]{1,0:T(8,128)S(1)} fusion(f32[24,128]{1,0:T(8,128)S(1)} %bitcast.99, f32[24,128]{1,0:T(8,128)S(1)} %bitcast.100, f32[24,128]{1,0:T(8,128)S(1)} %get-tuple-element.137, f32[24,128]{1,0:T(8,128)S(1)} %bitcast.101, f32[24,128]{1,0:T(8,128)S(1)} %get-tuple-element.139, f32[24,128]{1,0:T(8,128)S(1)} %bitcast.102, ...), kind=kLoop, calls=%fused_computation.2.clone.1 | loop fusion | flops 5108736 | bytes 110592 | tf_op jit(solution)/shard_map/while/body/eval_jaxpr/reduce_sum | solution.py:81
  117.7 2.2 %multiply_reduce_fusion.4 = f32[24,128]{1,0:T(8,128)S(1)} fusion(f32[24,128]{1,0:T(8,128)S(1)} %bitcast.99, f32[24,128]{1,0:T(8,128)S(1)} %bitcast.100, f32[24,128]{1,0:T(8,128)S(1)} %get-tuple-element.137, f32[24,128]{1,0:T(8,128)S(1)} %bitcast.101, f32[24,128]{1,0:T(8,128)S(1)} %get-tuple-element.139, f32[24,128]{1,0:T(8,128)S(1)} %bitcast.102, ...), kind=kLoop, calls=%fused_computation.2.clone.1 | loop fusion | flops 5108736 | bytes 110592 | tf_op jit(solution)/shard_map/while/body/eval_jaxpr/reduce_sum | solution.py:81
  148.3 2.2 %multiply_reduce_fusion.4 = f32[24,128]{1,0:T(8,128)S(1)} fusion(f32[24,128]{1,0:T(8,128)S(1)} %bitcast.99, f32[24,128]{1,0:T(8,128)S(1)} %bitcast.100, f32[24,128]{1,0:T(8,128)S(1)} %get-tuple-element.137, f32[24,128]{1,0:T(8,128)S(1)} %bitcast.101, f32[24,128]{1,0:T(8,128)S(1)} %get-tuple-element.139, f32[24,128]{1,0:T(8,128)S(1)} %bitcast.102, ...), kind=kLoop, calls=%fused_computation.2.clone.1 | loop fusion | flops 5108736 | bytes 110592 | tf_op jit(solution)/shard_map/while/body/eval_jaxpr/reduce_sum | solution.py:81
  154.6 9.5 %all-reduce.2 = (f32[8]{0:T(128)S(1)}, f32[]{:T(128)}, f32[]{:T(128)}, f32[8,8]{1,0:T(8,128)S(1)}) all-reduce(f32[8]{0:T(128)S(1)} %convolution_bitcast_fusion.2, f32[]{:T(128)S(6)} %mul.76, f32[]{:T(128)} %get-tuple-element.86, f32[8,8]{1,0:T(8,128)S(1)} %convolution_bitcast_fusion), channel_id=1, replica_groups=mesh['seg_0'=4,'seg_1'=4,'seg_2'=2,'grp'=4] {'seg_0'}, use_global_device_ids=true, to_apply=%region_3.4 | all-reduce | flops 74 | bytes 592 | tf_op jit(solution)/shard_map/psum | solution.py:65
  164.1 11.3 %all-reduce.1 = (f32[8]{0:T(128)S(1)}, f32[]{:T(128)}, f32[]{:T(128)}, f32[8,8]{1,0:T(8,128)S(1)}) all-reduce(f32[8]{0:T(128)S(1)} %get-tuple-element.76, f32[]{:T(128)} %get-tuple-element.77, f32[]{:T(128)} %get-tuple-element.78, f32[8,8]{1,0:T(8,128)S(1)} %get-tuple-element.79), channel_id=1, replica_groups=mesh['seg_0'=4,'seg_1'=4,'seg_2'=2,'grp'=4] {'seg_1'}, use_global_device_ids=true, to_apply=%region_4.5 | all-reduce | flops 74 | bytes 592 | tf_op jit(solution)/shard_map/psum | solution.py:65
  175.4 4.7 %all-reduce.3 = (f32[8]{0:T(128)S(1)}, f32[]{:T(128)}, f32[]{:T(128)}, f32[8,8]{1,0:T(8,128)S(1)}) all-reduce(f32[8]{0:T(128)S(1)} %get-tuple-element.72, f32[]{:T(128)} %get-tuple-element.73, f32[]{:T(128)} %get-tuple-element.74, f32[8,8]{1,0:T(8,128)S(1)} %get-tuple-element.75), channel_id=1, replica_groups=mesh['seg_0'=4,'seg_1'=4,'seg_2'=2,'grp'=4] {'seg_2'}, use_global_device_ids=true, to_apply=%region_5.6 | all-reduce | flops 74 | bytes 592 | tf_op jit(solution)/shard_map/psum | solution.py:65
  180.1 7.6 %all-reduce = (f32[8]{0:T(128)S(1)}, f32[]{:T(128)}, f32[]{:T(128)}, f32[8,8]{1,0:T(8,128)S(1)}) all-reduce(f32[8]{0:T(128)S(1)} %get-tuple-element.80, f32[]{:T(128)} %get-tuple-element.81, f32[]{:T(128)} %get-tuple-element.82, f32[8,8]{1,0:T(8,128)S(1)} %get-tuple-element.83), channel_id=1, replica_groups=mesh['seg_0'=4,'seg_1'=4,'seg_2'=2,'grp'=4] {'grp'}, use_global_device_ids=true, to_apply=%region_6.7 | all-reduce | flops 74 | bytes 592 | tf_op jit(solution)/shard_map/psum | solution.py:65
  (280 shorter events, 73.4 us)
Async XLA Ops:
  0.6 67.8 %copy-start = (bf16[24,128,121]{1,0,2:T(8,128)(2,1)S(1)}, bf16[24,128,121]{1,0,2:T(8,128)(2,1)}, u32[]{:S(2)}) copy-start(bf16[24,128,121]{1,0,2:T(8,128)(2,1)} %param.16) | copy-start | bytes 2230276
  0.6 10.3 %copy-start.2 = (f32[8,24,128]{2,1,0:T(8,128)S(1)}, f32[8,24,128]{2,1,0:T(8,128)}, u32[]{:S(2)}) copy-start(f32[8,24,128]{2,1,0:T(8,128)} %param.12) | copy-start | bytes 294916
  0.7 10.4 %copy-start.3 = (s32[24,189]{1,0:T(8,128)S(1)}, s32[24,189]{1,0:T(8,128)}, u32[]{:S(2)}) copy-start(s32[24,189]{1,0:T(8,128)} %param.20) | copy-start | bytes 54436
  0.7 24.3 %copy-start.5 = (s32[24,27]{1,0:T(8,128)S(1)}, s32[24,27]{1,0:T(8,128)}, u32[]{:S(2)}) copy-start(s32[24,27]{1,0:T(8,128)} %param.19) | copy-start | bytes 7780
  6.1 10.7 %all-to-all-start = ((f32[4,24,761]{2,1,0:T(8,128)}), f32[4,24,761]{2,1,0:T(8,128)S(1)}, u32[]{:S(2)}, u32[]{:S(2)}) async-start(f32[4,24,761]{2,1,0:T(8,128)} %broadcast_in_dim.39), calls=%async_computation | async-start | bytes 589824 | tf_op jit(solution)/shard_map/all_to_all | solution.py:20
  16.8 15.4 %collective-permute-start.3 = (f32[96,121]{1,0:T(8,128)S(1)}, f32[96,121]{1,0:T(8,128)S(1)}, u32[]{:S(2)}, u32[]{:S(2)}) collective-permute-start(f32[96,121]{1,0:T(8,128)S(1)} %split.9), channel_id=1, source_target_pairs={{4,0},{8,4},{12,8},{16,12},{20,16},{24,20},{28,24},{32,28},{36,32}... | collective-permute-start | bytes 139400 | tf_op jit(solution)/shard_map/ppermute | solution.py:56
  20.8 11.4 %collective-permute-start.2 = (f32[96,121]{1,0:T(8,128)S(1)}, f32[96,121]{1,0:T(8,128)S(1)}, u32[]{:S(2)}, u32[]{:S(2)}) collective-permute-start(f32[96,121]{1,0:T(8,128)S(1)} %split.9), channel_id=1, source_target_pairs={{0,4},{4,8},{8,12},{12,16},{16,20},{20,24},{24,28},{28,32},{32,36}... | collective-permute-start | bytes 139400 | tf_op jit(solution)/shard_map/ppermute | solution.py:54
  26.7 42.0 %collective-permute-start.1 = (f32[96,5,128]{0,2,1:T(8,128)}, f32[96,5,128]{0,2,1:T(8,128)}, u32[]{:S(2)}, u32[]{:S(2)}) collective-permute-start(f32[96,5,128]{0,2,1:T(8,128)} %bitcast.9), channel_id=1, source_target_pairs={{4,0},{8,4},{12,8},{16,12},{20,16},{24,20},{28,24},{32,28},{36,32}... | collective-permute-start | bytes 737288 | tf_op jit(solution)/shard_map/ppermute | solution.py:56
  28.6 40.1 %collective-permute-start = (f32[96,5,128]{0,2,1:T(8,128)}, f32[96,5,128]{0,2,1:T(8,128)}, u32[]{:S(2)}, u32[]{:S(2)}) collective-permute-start(f32[96,5,128]{0,2,1:T(8,128)} %bitcast.9), channel_id=1, source_target_pairs={{0,4},{4,8},{8,12},{12,16},{16,20},{20,24},{24,28},{28,32},{32,36}... | collective-permute-start | bytes 737288 | tf_op jit(solution)/shard_map/ppermute | solution.py:54
  39.8 1.6 copy-start.4
  68.7 2.2 %copy-start.1 = (f32[24,3,128]{2,0,1:T(8,128)S(1)}, f32[24,3,128]{2,0,1:T(8,128)}, u32[]{:S(2)}) copy-start(f32[24,3,128]{2,0,1:T(8,128)} %param.13) | copy-start | bytes 110596
where the time goes:
time: 195 us; the launch traced here: 194 us
  other arithmetic  71.5 us (37%)
  blocking collectives  33.1 us (17%)
  matrix products  30.5 us (16%)
  local copies, waits for them, and re-layouts  28.4 us (15%)
  starting transfers between devices  17.8 us (9%)
  waiting for transfers between devices  5.32 us (3%)
  between operations  4.91 us (3%)
  loops' own time  2.26 us (1%)
    reduce_sum x27, other arithmetic, near_step(): return (running + jnp.sum(kernel * source[:, 4, None, :], axis=2), None)  59.9 us
    psum x4, blocking collectives, by_axis(): value = lax.psum(value, axis)  33.1 us
    dot_general x1, matrix products, far_field(): jnp.einsum('tok,oik->ti', summed, m2l.astype(jnp.float32), precision=high...  16.4 us
    gather x27, local copies, waits for them, and re-layouts, near_step(): source = jnp.take(wide_panels, column, axis=0)  15.6 us
    dot_general x1, matrix products, far_field(): summed = jnp.einsum('tfo,tfk->tok', offset_hot, gathered, precision=highest)  10.6 us
    gather x2, local copies, waits for them, and re-layouts, far_field(): gathered = jnp.take(wide_poles, far_list, axis=0)  9 us
    ppermute x2, starting transfers between devices, with_halo(): lax.ppermute(tail, axis, [(i, (i + 1) % count) for i in range(ends)])  7.09 us
    ppermute x2, starting transfers between devices, with_halo(): lax.ppermute(head, axis, [((i + 1) % count, i) for i in range(ends)])  5.91 us
  transfers between devices with their start and end apart: 5, of which 1 were waited for; matrix products, arithmetic and copies ran while one was open for 20% of the time, Pallas kernels for 0%

commit v1 on v0

v1 whole, which is shorter than its diff:
```python
import math

import jax
import jax.numpy as jnp
from jax import lax
from jax.experimental import pallas as pl
from jax.experimental.pallas import tpu as pltpu
from jax.sharding import Mesh
from jax.sharding import PartitionSpec as P

Y, Z, C, X = "seg_0", "seg_1", "seg_2", "grp"
AXES = (Y, Z, C, X)
MESH = pl.DeviceIdType.MESH
NT = (((1,), (1,)), ((), ()))
four_pi = 12.566370614359172
epsilon = 1e-06
f32 = jnp.float32
bf16 = jnp.bfloat16


def round_up(value, step):
    return -(-value // step) * step


def high_low(value):
    high = value.astype(bf16).astype(f32)
    return high, value - high


def two_parts(value):
    high, low = high_low(value)
    return high, low.astype(bf16).astype(f32)


def make_step(sizes, krylov, leaves, panels, terms, offsets, near, far):
    ny, nz, nc, nx = sizes
    segments = ny * nz * nc
    window = 3 * nx * leaves
    wide = round_up(window, 128)
    off_pad = round_up(offsets, 16)
    far_pad = round_up(far, 128)
    lanes = 128
    group_a = nx * nc
    group_b = ny * nz
    rows = 16

    def kernel(
        basis_ref, coords_ref, areas_ref, counts_ref, near_ref, far_ref, off_ref,
        p2m_hbm, l2p_hbm, m2l_hbm,
        vec_ref, hess_ref,
        p2m_v, l2p_v, m2l_v, panels_v, poles_v, far_v, off_v, count_v, sum_v, left_v,
        right_v, weight_v, part_v, near_v, stage_a, stage_b,
        load_sem, pole_send, pole_recv, panel_send, panel_recv, a_send, a_recv, b_send, b_recv,
    ):
        y, z, c, x = (lax.axis_index(name) for name in AXES)
        q = y * nz + z
        seg = q * nc + c
        q_across = lax.rem(q + group_b - 1 + 2 * c, group_b)
        y_across, z_across = q_across // nz, lax.rem(q_across, nz)

        loads = [
            pltpu.make_async_copy(src, dst, load_sem.at[k])
            for k, (src, dst) in enumerate(((p2m_hbm, p2m_v), (m2l_hbm, m2l_v), (l2p_hbm, l2p_v)))
        ]
        for load in loads:
            load.start()

        def ring(step):
            return lax.rem(x + step, nx)

        partner = (y, z, 1 - c, x)
        across = (y_across, z_across, 1 - c, x)
        peers_a = [(y, z, c, ring(r)) for r in range(1, nx)]
        peers_a += [(y, z, 1 - c, ring(r)) for r in range(nx)]
        peers_b = []
        for r in range(1, group_b):
            other = lax.rem(q + r, group_b)
            peers_b.append((other // nz, lax.rem(other, nz), c, x))

        barrier = pltpu.get_barrier_semaphore()
        everyone = peers_a + peers_b + [across]
        for peer in everyone:
            pl.semaphore_signal(barrier, inc=1, device_id=peer, device_id_type=MESH)

        slot_rows = lax.broadcasted_iota(jnp.int32, (leaves, panels), 0)
        mask = (slot_rows < counts_ref[0]).astype(f32)
        current = basis_ref[krylov - 1] * mask
        own = nx + x
        for comp in range(3):
            panels_v[own, comp] = coords_ref[:, comp, :]
        panels_v[own, 3] = areas_ref[...]
        panels_v[own, 4] = current

        padded = round_up(leaves, 16)

        def tall(value):
            extra = jnp.zeros((padded - leaves, value.shape[1]), f32)
            return jnp.concatenate([value, extra], axis=0).astype(bf16)

        rounded = tall(current)
        loads[0].wait()

        def to_poles(t, running):
            product = lax.dot_general(rounded, p2m_v[t], NT, preferred_element_type=f32)
            row = lax.broadcasted_iota(jnp.int32, product.shape, 0)
            return jnp.where(row == t, product, running)

        multipoles = lax.fori_loop(0, leaves, to_poles, jnp.zeros((padded, terms), f32))
        poles_v[own] = jnp.zeros((leaves, lanes), f32)
        poles_v[own, :, :terms] = multipoles[:leaves]

        pl.semaphore_wait(barrier, len(everyone))

        def send(buffer, sends, recvs, number, source, target_slot, peer):
            copy = pltpu.make_async_remote_copy(
                src_ref=buffer.at[source],
                dst_ref=buffer.at[target_slot],
                send_sem=sends.at[number],
                recv_sem=recvs.at[target_slot],
                device_id=peer,
                device_id_type=MESH,
            )
            copy.start()
            return copy

        sent = []

        def first_sends(buffer, sends, recvs):
            for r in range(1, nx):
                sent.append(send(buffer, sends, recvs, r - 1, own, own, (y, z, c, ring(r))))
            base = nx - 1
            sent.append(send(buffer, sends, recvs, base, own, 2 * nx * c + x, partner))
            sent.append(send(buffer, sends, recvs, base + 1, own, 2 * nx * (1 - c) + x, across))

        def received(buffer, sends, recvs, slot):
            pltpu.make_async_remote_copy(
                src_ref=buffer.at[slot],
                dst_ref=buffer.at[slot],
                send_sem=sends.at[0],
                recv_sem=recvs.at[slot],
                device_id=partner,
                device_id_type=MESH,
            ).wait_recv()

        def forward(buffer, sends, recvs, r):
            other = ring(r)
            received(buffer, sends, recvs, nx + other)
            base = nx + 1 + 2 * (r - 1)
            sent.append(send(buffer, sends, recvs, base, nx + other, 2 * nx * c + other, partner))
            sent.append(
                send(buffer, sends, recvs, base + 1, nx + other, 2 * nx * (1 - c) + other, across)
            )

        pole_set = (poles_v, pole_send, pole_recv)
        panel_set = (panels_v, panel_send, panel_recv)
        first_sends(*pole_set)
        first_sends(*panel_set)

        far_v[...] = jnp.full(far_v.shape, -1, jnp.int32)
        off_v[...] = jnp.full(off_v.shape, -1, jnp.int32)
        far_v[:, :far] = far_ref[...]
        off_v[:, :far] = off_ref[...]

        def to_counts(t, carry):
            off_row = jnp.broadcast_to(off_v[pl.ds(t, 1), :], (off_pad, far_pad))
            far_row = jnp.broadcast_to(far_v[pl.ds(t, 1), :], (wide, far_pad))
            off_hot = lax.broadcasted_iota(jnp.int32, (off_pad, far_pad), 0) == off_row
            far_hot = lax.broadcasted_iota(jnp.int32, (wide, far_pad), 0) == far_row
            pairs = lax.dot_general(
                jnp.where(off_hot, 1.0, 0.0).astype(bf16),
                jnp.where(far_hot, 1.0, 0.0).astype(bf16),
                NT,
                preferred_element_type=f32,
            )
            count_v[t] = pairs.astype(bf16)
            return carry

        lax.fori_loop(0, leaves, to_counts, 0)

        for r in (1, nx - 1, nx // 2):
            forward(*pole_set, r)

        left_v[...] = jnp.zeros(left_v.shape, bf16)
        own_comps = [panels_v[own, comp] - 2.0 for comp in range(3)]
        splits = [two_parts(value) for value in own_comps]
        norm = sum((value[0] + value[1]) * (value[0] + value[1]) for value in splits)
        norm_high, norm_low = high_low(norm)
        one = jnp.ones((leaves, panels), f32)
        zero = jnp.zeros((leaves, panels), f32)
        highs = [-2.0 * value[0] for value in splits]
        lows = [-2.0 * value[1] for value in splits]
        columns = highs + [one, one, one, norm_high, zero]
        columns += highs + [zero] * 5
        columns += lows + [zero, zero, zero, norm_low, zero]
        columns += lows + [zero] * 5
        for k, column in enumerate(columns):
            part_v[pl.ds(k, leaves, stride=2 * rows), :] = column

        def to_left(t, carry):
            block = part_v[pl.ds(pl.multiple_of(t * 2 * rows, 2 * rows), 2 * rows), :]
            left_v[t, :, : 2 * rows] = block.T.astype(bf16)
            return carry

        lax.fori_loop(0, leaves, to_left, 0)

        for r in (1, nx - 1, nx // 2):
            forward(*panel_set, r)

        tile_lane = lax.broadcasted_iota(jnp.int32, (krylov, lanes), 1)
        masked = [basis_ref[j] * mask for j in range(krylov)]

        def folded(value):
            return sum(value[8 * k : 8 * k + 8] for k in range(leaves // 8))

        def full_sum(value):
            return jnp.sum(jnp.sum(value, axis=0, keepdims=True), axis=1, keepdims=True)

        def inner_products(vector):
            lines = [
                jnp.sum(folded(masked[i] * vector), axis=0, keepdims=True) for i in range(krylov)
            ]
            return jnp.sum(jnp.concatenate(lines, axis=0), axis=1, keepdims=True)

        tile = jnp.zeros((krylov, lanes), f32)
        for j in range(krylov):
            tile = jnp.where(tile_lane == j, inner_products(masked[j]), tile)
        tile = jnp.where(tile_lane == krylov + 2, full_sum(folded(mask)), tile)

        valid_before = (seg > 0).astype(f32)
        valid_after = (seg < segments - 1).astype(f32)

        def outside_slots(recv):
            for k in range(nx):
                recv(k)
                recv(2 * nx + k)

        outside_slots(lambda slot: received(*pole_set, slot))

        pole_parts = []
        for slot in range(3 * nx):
            value = poles_v[slot]
            if slot < nx:
                value = value * valid_before
            if slot >= 2 * nx:
                value = value * valid_after
            pole_parts.append(value)
        pole_parts.append(jnp.zeros((wide - window, lanes), f32))
        all_poles = jnp.concatenate(pole_parts, axis=0)
        pole_high, pole_low = high_low(all_poles)
        both_poles = jnp.concatenate([pole_high, pole_low], axis=1).astype(bf16)

        def to_sums(t, carry):
            both = jnp.dot(count_v[t], both_poles, preferred_element_type=f32)
            start = pl.multiple_of(t * off_pad, off_pad)
            sum_v[pl.ds(start, off_pad), :] = both[:, :lanes] + both[:, lanes:]
            return carry

        lax.fori_loop(0, leaves, to_sums, 0)

        loads[1].wait()

        def to_local(o, running):
            sums = sum_v[pl.ds(o, leaves, stride=off_pad), :]
            high, low = high_low(sums)
            stacked = jnp.concatenate([high, low], axis=0).astype(bf16)
            return running + lax.dot_general(
                stacked[:, :terms], m2l_v[o], NT, preferred_element_type=f32
            )

        both = lax.fori_loop(
            0, offsets, to_local, jnp.zeros((2 * leaves, terms), f32), unroll=4
        )
        local = tall(both[:leaves] + both[leaves:])
        loads[2].wait()

        def to_distant(t, running):
            product = lax.dot_general(local, l2p_v[t], NT, preferred_element_type=f32)
            row = lax.broadcasted_iota(jnp.int32, product.shape, 0)
            return jnp.where(row == t, product, running)

        distant = lax.fori_loop(0, leaves, to_distant, jnp.zeros((padded, panels), f32))[:leaves]

        outside_slots(lambda slot: received(*panel_set, slot))

        for slot in range(3 * nx):
            parts = [two_parts(panels_v[slot, comp] - 2.0) for comp in range(3)]
            area = panels_v[slot, 3]
            weight = area * panels_v[slot, 4] * (1.0 / four_pi)
            if slot < nx:
                weight = weight * valid_before
            if slot >= 2 * nx:
                weight = weight * valid_after
            square = sum((value[0] + value[1]) * (value[0] + value[1]) for value in parts)
            first, rest = high_low(square + area)
            second, third = high_low(rest)
            lines = [value[0] for value in parts] + [first, second, third, one, zero]
            lines += [value[1] for value in parts] + [zero] * 5
            for k, line in enumerate(lines):
                right_v[slot * leaves : (slot + 1) * leaves, k, :] = line
            weight_v[slot * leaves : (slot + 1) * leaves, 0, :] = weight

        near_v[...] = jnp.zeros(near_v.shape, f32)
        pair_lane = lax.broadcasted_iota(jnp.int32, (panels, lanes), 1)

        def to_near(t, carry):
            left = left_v[t]
            running = jnp.zeros((panels, panels), f32)
            for start in range(0, near, 2):
                entries = [near_ref[t, n] for n in range(start, min(start + 2, near))]
                blocks = []
                for w in entries:
                    block = right_v[w].astype(bf16)
                    fill = jnp.zeros((lanes - 2 * rows, panels), bf16)
                    blocks.append(jnp.concatenate([block, block, fill], axis=0))
                right = jnp.concatenate(blocks, axis=1) if len(blocks) > 1 else blocks[0]
                square = jnp.dot(left, right, preferred_element_type=f32)
                for k, w in enumerate(entries):
                    inverse = lax.rsqrt(square[:, k * panels : (k + 1) * panels])
                    running = running + inverse * weight_v[w]
            total = jnp.sum(running, axis=1, keepdims=True)
            near_v[...] = jnp.where(pair_lane == t, total, near_v[...])
            return carry

        lax.fori_loop(0, leaves, to_near, 0)
        nearby = near_v[...].T[:leaves]

        image = (0.5 * current + nearby + distant) * mask
        tile = jnp.where(tile_lane == krylov, inner_products(image), tile)
        tile = jnp.where(tile_lane == krylov + 1, full_sum(folded(image * image)), tile)

        def exchange(stage, sends, recvs, me, others, value):
            stage[me] = value
            copies = []
            for k, (slot, peer) in enumerate(others):
                copy = pltpu.make_async_remote_copy(
                    src_ref=stage.at[me],
                    dst_ref=stage.at[me],
                    send_sem=sends.at[k],
                    recv_sem=recvs.at[me],
                    device_id=peer,
                    device_id_type=MESH,
                )
                copy.start()
                copies.append(copy)
            for slot, peer in others:
                pltpu.make_async_remote_copy(
                    src_ref=stage.at[slot],
                    dst_ref=stage.at[slot],
                    send_sem=sends.at[0],
                    recv_sem=recvs.at[slot],
                    device_id=peer,
                    device_id_type=MESH,
                ).wait_recv()
            total = stage[0]
            for k in range(1, stage.shape[0]):
                total = total + stage[k]
            sent.extend(copies)
            return total

        others_a = [(ring(r) * nc + c, (y, z, c, ring(r))) for r in range(1, nx)]
        others_a += [(ring(r) * nc + 1 - c, (y, z, 1 - c, ring(r))) for r in range(nx)]
        tile = exchange(stage_a, a_send, a_recv, x * nc + c, others_a, tile)
        others_b = [(lax.rem(q + r, group_b), peers_b[r - 1]) for r in range(1, group_b)]
        tile = exchange(stage_b, b_send, b_recv, q, others_b, tile)

        def column(index):
            return jnp.sum(jnp.where(tile_lane == index, tile, 0.0), axis=1, keepdims=True)

        population = column(krylov + 2)[:1]
        products = column(krylov)
        energy = column(krylov + 1)[:1]
        coefficients = products / population
        tile_row = lax.broadcasted_iota(jnp.int32, (krylov, lanes), 0)
        spread = jnp.sum(
            jnp.where(tile_lane == tile_row, coefficients, 0.0), axis=0, keepdims=True
        )
        gram = jnp.where(tile_lane < krylov, tile, 0.0)
        curvature = full_sum(gram * coefficients * spread)
        squares = energy - 2.0 * full_sum(coefficients * products) + curvature
        scale = jnp.sqrt(squares / population + epsilon)
        residue = image
        for j in range(krylov):
            residue = residue - coefficients[j : j + 1] * masked[j]
        vec_ref[...] = residue / scale
        lane_row = lax.broadcasted_iota(jnp.int32, (1, lanes), 1)
        hess_ref[...] = jnp.where(lane_row == krylov, scale, spread)

        for copy in sent:
            copy.wait_send()

    vmem = pl.BlockSpec(memory_space=pltpu.VMEM)
    smem = pl.BlockSpec(memory_space=pltpu.SMEM)
    anywhere = pl.BlockSpec(memory_space=pl.ANY)
    dma = pltpu.SemaphoreType.DMA
    slots = 3 * nx
    n_sends = nx + 1 + 2 * (nx - 1)
    return pl.pallas_call(
        kernel,
        out_shape=(
            jax.ShapeDtypeStruct((leaves, panels), f32),
            jax.ShapeDtypeStruct((1, lanes), f32),
        ),
        in_specs=[vmem, vmem, vmem, smem, smem, vmem, vmem, anywhere, anywhere, anywhere],
        out_specs=(vmem, vmem),
        scratch_shapes=[
            pltpu.VMEM((leaves, terms, panels), bf16),
            pltpu.VMEM((leaves, panels, terms), bf16),
            pltpu.VMEM((offsets, terms, terms), bf16),
            pltpu.VMEM((slots, 5, leaves, panels), f32),
            pltpu.VMEM((slots, leaves, lanes), f32),
            pltpu.VMEM((leaves, far_pad), jnp.int32),
            pltpu.VMEM((leaves, far_pad), jnp.int32),
            pltpu.VMEM((leaves, off_pad, wide), bf16),
            pltpu.VMEM((leaves * off_pad, lanes), f32),
            pltpu.VMEM((leaves, panels, lanes), bf16),
            pltpu.VMEM((window, rows, panels), f32),
            pltpu.VMEM((window, 1, panels), f32),
            pltpu.VMEM((leaves * 2 * rows, panels), f32),
            pltpu.VMEM((panels, lanes), f32),
            pltpu.VMEM((group_a, krylov, lanes), f32),
            pltpu.VMEM((group_b, krylov, lanes), f32),
            dma((3,)),
            dma((n_sends,)),
            dma((slots,)),
            dma((n_sends,)),
            dma((slots,)),
            dma((group_a,)),
            dma((group_a,)),
            dma((group_b,)),
            dma((group_b,)),
        ],
        compiler_params=pltpu.CompilerParams(
            collective_id=0, has_side_effects=True, vmem_limit_bytes=56 * 1024 * 1024
        ),
    )


def solution(mesh):
    torus = Mesh(mesh.devices.reshape(4, 4, 2, mesh.shape["grp"]), AXES)
    every = AXES

    def on_device(basis, coords, areas, p2m, l2p, m2l, counts, near_list, far_list, far_offset):
        krylov, leaves, panels = basis.shape
        step = make_step(
            torus.devices.shape, krylov, leaves, panels, p2m.shape[1], m2l.shape[0],
            near_list.shape[1], far_list.shape[1],
        )
        vector, hessenberg = step(
            basis, coords, areas, counts, near_list, far_list, far_offset, p2m, l2p, m2l
        )
        return vector, hessenberg[0, : krylov + 1]

    in_specs = (
        P(None, every, None),
        P(every, None, None),
        P(every, None),
        P(every, None, None),
        P(every, None, None),
        P(),
        P(every),
        P(every, None),
        P(every, None),
        P(every, None),
    )
    out_specs = (P(every, None), P())
    return jax.shard_map(
        on_device, mesh=torus, in_specs=in_specs, out_specs=out_specs, check_vma=False
    )
```

time: 195 us -> 93.6 us (0.48)
  other arithmetic: 71.5 us -> 0 us
  Pallas kernels: 0 us -> 69.2 us
  blocking collectives: 33.1 us -> 0 us
  matrix products: 30.5 us -> 0 us
  starting transfers between devices: 17.8 us -> 0 us
  local copies, waits for them, and re-layouts: 28.4 us -> 22.6 us
  waiting for transfers between devices: 5.32 us -> 0 us
  between operations: 4.91 us -> 1.29 us
  loops' own time: 2.26 us -> 0 us
    pallas_call x0 -> x1, Pallas kernels: none -> 69.2 us  [on_device(): step(basis, coords, areas, counts, near_list, far_list, far_offset, p2m,...]
    reduce_sum x29 -> x0, other arithmetic: 61.2 us -> none  [the longest x27 59.9 us: near_step(): return (running + jnp.sum(kernel * source[:, 4, None, :], axis=2), None)]
    psum x4 -> x0, blocking collectives: 33.1 us -> none  [by_axis(): value = lax.psum(value, axis)]
    dot_general x8 -> x0, matrix products: 30.5 us -> none  [the longest x1 16.4 us: far_field(): jnp.einsum('tok,oik->ti', summed, m2l.astype(jnp.float32), precision=high...]
    gather x29 -> x0, local copies, waits for them, and re-layouts: 24.6 us -> none  [the longest x27 15.6 us: near_step(): source = jnp.take(wide_panels, column, axis=0)]
    unnamed x14 -> x5, local copies, waits for them, and re-layouts: 0.66 us -> 21.5 us
    ppermute x4 -> x0, starting transfers between devices: 13 us -> none  [the longest x2 7.09 us: with_halo(): lax.ppermute(tail, axis, [(i, (i + 1) % count) for i in range(ends)])]
    all_to_all x1 -> x0, waiting for transfers between devices: 5.31 us -> none  [from_everyone(): return lax.all_to_all(copies, axis, split_axis=0, concat_axis=0, tiled=True)]
  transfers between devices with their start and end apart: 5 -> 0, of which waited for: 1 -> 0; matrix products, arithmetic and copies ran while one was open for 20% -> 0% of each run, Pallas kernels for 0% -> 0%
where the time goes in v1:
time: 93.6 us; the launch traced here: 93.2 us
  Pallas kernels  69.2 us (74%)
  local copies, waits for them, and re-layouts  22.6 us (24%)
  between operations  1.29 us (1%)
    pallas_call x1, Pallas kernels, on_device(): step(basis, coords, areas, counts, near_list, far_list, far_offset, p2m,...  69.2 us
    unnamed x5, local copies, waits for them, and re-layouts  21.5 us

profile of v1, /device:TPU:1, one launch (start us, length us, event | category | flops | bytes accessed | tf_op | source)
XLA Modules:
  0.0 93.2 jit_solution(13572086835819056493)
XLA Ops:
  1.3 1.4 %copy.12.coords_ref = f32[24,3,128]{2,1,0:T(4,128)} copy(f32[24,3,128]{2,0,1:T(8,128)} %param.11) | data formatting | bytes 73728 | tf_op args[1]
  2.7 2.2 %copy.13.p2m_hbm = bf16[24,121,128]{2,1,0:T(8,128)(2,1)} copy(bf16[24,121,128]{2,0,1:T(8,128)(2,1)} %param.13) | data formatting | bytes 1486848 | tf_op args[3]
  4.9 2.4 %copy.14.l2p_hbm = bf16[24,128,121]{2,1,0:T(8,128)(2,1)} copy(bf16[24,128,121]{1,0,2:T(8,128)(2,1)} %param.14) | data formatting | bytes 1486848 | tf_op args[4]
  7.3 14.2 %copy.15.m2l_hbm = bf16[316,121,121]{2,1,0:T(8,128)(2,1)} copy(bf16[316,121,121]{2,0,1:T(8,128)(2,1)} %param.15) | data formatting | bytes 18506224 | tf_op args[5]
  21.5 69.2 %shard_map.113 = (f32[24,128]{1,0:T(8,128)}, f32[1,128]{1,0:T(1,128)}) custom-call(f32[8,24,128]{2,1,0:T(8,128)} %basis_ref.1, f32[24,3,128]{2,1,0:T(4,128)} %copy.12.coords_ref, f32[24,128]{1,0:T(8,128)} %areas_ref.1, s32[1]{0:T(128)S(6)} %copy.17.counts_ref, s32[24,27]{1,0:T(8,128)} %near_ref.1, s32[24,189]{1,0:T(8,128)} %far_ref.1, s32[24,189]{1,0:T(8,128)} %off_ref.1, ...), custom_call_target="tpu_custom_call" | custom-call | tf_op jit(solution)/shard_map/pallas_call | solution.py:448
  90.7 1.1 %slice_bitcast_fusion = f32[9]{0:T(128)} fusion(f32[1,128]{1,0:T(1,128)} %get-tuple-element.5), kind=kLoop, calls=%fused_computation | loop fusion | bytes 72 | tf_op jit(solution)/shard_map/squeeze | solution.py:451
  91.9 1.3 %copy.18 = f32[24,128]{1,0:T(8,128)} copy(f32[24,128]{1,0:T(8,128)} %get-tuple-element.8) | data formatting | bytes 24576

commit v2 on v1

--- a/solution.py
+++ b/solution.py
@@ -38,18 +38,23 @@
     window = 3 * nx * leaves
     wide = round_up(window, 128)
     off_pad = round_up(offsets, 16)
+    off_step = off_pad + 8
     far_pad = round_up(far, 128)
     lanes = 128
     group_a = nx * nc
     group_b = ny * nz
     rows = 16
+    row_step = 24
+    part_step = 40
+    group = 8
+    folded_rows = group * lanes
 
     def kernel(
         basis_ref, coords_ref, areas_ref, counts_ref, near_ref, far_ref, off_ref,
         p2m_hbm, l2p_hbm, m2l_hbm,
         vec_ref, hess_ref,
         p2m_v, l2p_v, m2l_v, panels_v, poles_v, far_v, off_v, count_v, sum_v, left_v,
-        right_v, weight_v, part_v, near_v, stage_a, stage_b,
+        right_v, part_v, near_v, p2m_f, l2p_f, m2l_f, stage_a, stage_b,
         load_sem, pole_send, pole_recv, panel_send, panel_recv, a_send, a_recv, b_send, b_recv,
     ):
         y, z, c, x = (lax.axis_index(name) for name in AXES)
@@ -87,7 +92,7 @@
         current = basis_ref[krylov - 1] * mask
         own = nx + x
         for comp in range(3):
-            panels_v[own, comp] = coords_ref[:, comp, :]
+            panels_v[own, comp] = coords_ref[comp]
         panels_v[own, 3] = areas_ref[...]
         panels_v[own, 4] = current
 
@@ -100,14 +105,40 @@
         rounded = tall(current)
         loads[0].wait()
 
-        def to_poles(t, running):
-            product = lax.dot_general(rounded, p2m_v[t], NT, preferred_element_type=f32)
-            row = lax.broadcasted_iota(jnp.int32, product.shape, 0)
-            return jnp.where(row == t, product, running)
-
-        multipoles = lax.fori_loop(0, leaves, to_poles, jnp.zeros((padded, terms), f32))
+        def unfold(source, scratch, part, count):
+            block = source[:, pl.ds(pl.multiple_of(part * group, group), count), :].astype(f32)
+            width = block.shape[2]
+            if count == group:
+                scratch[: block.shape[0] * group, :width] = block.reshape(-1, width)
+            else:
+                for k in range(block.shape[0]):
+                    scratch[k * group : k * group + count, :width] = block[k]
+
+        def unfolded(scratch, k):
+            return scratch[pl.ds(k, lanes, stride=group), :].astype(bf16)
+
+        def per_leaf(values, source, scratch, dims, running):
+            def one_group(part, running):
+                unfold(source, scratch, part, group)
+                for k in range(group):
+                    product = lax.dot_general(
+                        values, unfolded(scratch, k), dims, preferred_element_type=f32
+                    )
+                    row = lax.broadcasted_iota(jnp.int32, product.shape, 0)
+                    running = jnp.where(row == part * group + k, product, running)
+                return running
+
+            return lax.fori_loop(0, leaves // group, one_group, running)
+
+        blank = jnp.zeros((padded, lanes), f32)
+        multipoles = per_leaf(rounded, p2m_v, p2m_f, NT, blank)
         poles_v[own] = jnp.zeros((leaves, lanes), f32)
-        poles_v[own, :, :terms] = multipoles[:leaves]
+        poles_v[own, :, :terms] = multipoles[:leaves, :terms]
+
+        pattern = (lax.broadcasted_iota(jnp.int32, (window, rows, panels), 1) == 6).astype(f32)
+        right_v[:, :rows, :] = pattern
+        for scratch in (l2p_f, m2l_f):
+            scratch[...] = jnp.zeros(scratch.shape, f32)
 
         pl.semaphore_wait(barrier, len(everyone))
 
@@ -175,10 +206,15 @@
             count_v[t] = pairs.astype(bf16)
             return carry
 
-        lax.fori_loop(0, leaves, to_counts, 0)
-
-        for r in (1, nx - 1, nx // 2):
-            forward(*pole_set, r)
+        third = leaves // 4
+        lax.fori_loop(0, 2 * third, to_counts, 0, unroll=2)
+        forward(*pole_set, 1)
+        forward(*pole_set, nx - 1)
+        lax.fori_loop(2 * third, 3 * third, to_counts, 0, unroll=2)
+        forward(*pole_set, nx // 2)
+        forward(*panel_set, 1)
+        forward(*panel_set, nx - 1)
+        lax.fori_loop(3 * third, leaves, to_counts, 0, unroll=2)
 
         left_v[...] = jnp.zeros(left_v.shape, bf16)
         own_comps = [panels_v[own, comp] - 2.0 for comp in range(3)]
@@ -194,17 +230,15 @@
         columns += lows + [zero, zero, zero, norm_low, zero]
         columns += lows + [zero] * 5
         for k, column in enumerate(columns):
-            part_v[pl.ds(k, leaves, stride=2 * rows), :] = column
+            part_v[pl.ds(k, leaves, stride=part_step), :] = column
 
         def to_left(t, carry):
-            block = part_v[pl.ds(pl.multiple_of(t * 2 * rows, 2 * rows), 2 * rows), :]
+            block = part_v[pl.ds(pl.multiple_of(t * part_step, 8), 2 * rows), :]
             left_v[t, :, : 2 * rows] = block.T.astype(bf16)
             return carry
 
-        lax.fori_loop(0, leaves, to_left, 0)
-
-        for r in (1, nx - 1, nx // 2):
-            forward(*panel_set, r)
+        lax.fori_loop(0, leaves, to_left, 0, unroll=4)
+        forward(*panel_set, nx // 2)
 
         tile_lane = lax.broadcasted_iota(jnp.int32, (krylov, lanes), 1)
         masked = [basis_ref[j] * mask for j in range(krylov)]
@@ -251,34 +285,48 @@
 
         def to_sums(t, carry):
             both = jnp.dot(count_v[t], both_poles, preferred_element_type=f32)
-            start = pl.multiple_of(t * off_pad, off_pad)
+            start = pl.multiple_of(t * off_step, 8)
             sum_v[pl.ds(start, off_pad), :] = both[:, :lanes] + both[:, lanes:]
             return carry
 
-        lax.fori_loop(0, leaves, to_sums, 0)
+        lax.fori_loop(0, leaves, to_sums, 0, unroll=2)
 
         loads[1].wait()
 
-        def to_local(o, running):
-            sums = sum_v[pl.ds(o, leaves, stride=off_pad), :]
-            high, low = high_low(sums)
-            stacked = jnp.concatenate([high, low], axis=0).astype(bf16)
-            return running + lax.dot_general(
-                stacked[:, :terms], m2l_v[o], NT, preferred_element_type=f32
-            )
-
-        both = lax.fori_loop(
-            0, offsets, to_local, jnp.zeros((2 * leaves, terms), f32), unroll=4
-        )
-        local = tall(both[:leaves] + both[leaves:])
+        def add_local(part, half, count, running):
+            scratch = m2l_f.at[half]
+            unfold(m2l_v, scratch, part, count)
+            for k in range(0, count, 2):
+                lefts, rights = [], []
+                for o in (k, k + 1):
+                    sums = sum_v[pl.ds(part * group + o, leaves, stride=off_step), :]
+                    high, low = high_low(sums)
+                    lefts.append(jnp.concatenate([high, low], axis=0).astype(bf16))
+                    rights.append(unfolded(scratch, o))
+                running = running + lax.dot_general(
+                    jnp.concatenate(lefts, axis=1),
+                    jnp.concatenate(rights, axis=1),
+                    NT,
+                    preferred_element_type=f32,
+                )
+            return running
+
+        def to_local(step, running):
+            for half in range(2):
+                running = add_local(2 * step + half, half, group, running)
+            return running
+
+        whole = offsets // group
+        both = lax.fori_loop(0, whole // 2, to_local, jnp.zeros((2 * leaves, lanes), f32))
+        for part in range(whole // 2 * 2, whole):
+            both = add_local(part, 0, group, both)
+        if offsets % group:
+            both = add_local(whole, 1, offsets % group, both)
+        inside = lax.broadcasted_iota(jnp.int32, (leaves, lanes), 1) < terms
+        local = tall(jnp.where(inside, both[:leaves] + both[leaves:], 0.0))
         loads[2].wait()
-
-        def to_distant(t, running):
-            product = lax.dot_general(local, l2p_v[t], NT, preferred_element_type=f32)
-            row = lax.broadcasted_iota(jnp.int32, product.shape, 0)
-            return jnp.where(row == t, product, running)
-
-        distant = lax.fori_loop(0, leaves, to_distant, jnp.zeros((padded, panels), f32))[:leaves]
+        plain = (((1,), (0,)), ((), ()))
+        distant = per_leaf(local, l2p_v, l2p_f, plain, blank)[:leaves]
 
         outside_slots(lambda slot: received(*panel_set, slot))
 
@@ -293,11 +341,12 @@
             square = sum((value[0] + value[1]) * (value[0] + value[1]) for value in parts)
             first, rest = high_low(square + area)
             second, third = high_low(rest)
-            lines = [value[0] for value in parts] + [first, second, third, one, zero]
-            lines += [value[1] for value in parts] + [zero] * 5
-            for k, line in enumerate(lines):
-                right_v[slot * leaves : (slot + 1) * leaves, k, :] = line
-            weight_v[slot * leaves : (slot + 1) * leaves, 0, :] = weight
+            lines = [value[0] for value in parts] + [first, second, third]
+            lines = list(enumerate(lines)) + [(7, weight)]
+            lines += [(8 + k, value[1]) for k, value in enumerate(parts)]
+            flat = right_v.reshape(window * row_step, panels)
+            for k, line in lines:
+                flat[pl.ds(slot * leaves * row_step + k, leaves, stride=row_step), :] = line
 
         near_v[...] = jnp.zeros(near_v.shape, f32)
         pair_lane = lax.broadcasted_iota(jnp.int32, (panels, lanes), 1)
@@ -309,19 +358,19 @@
                 entries = [near_ref[t, n] for n in range(start, min(start + 2, near))]
                 blocks = []
                 for w in entries:
-                    block = right_v[w].astype(bf16)
+                    block = right_v[w, :rows, :].astype(bf16)
                     fill = jnp.zeros((lanes - 2 * rows, panels), bf16)
                     blocks.append(jnp.concatenate([block, block, fill], axis=0))
                 right = jnp.concatenate(blocks, axis=1) if len(blocks) > 1 else blocks[0]
                 square = jnp.dot(left, right, preferred_element_type=f32)
                 for k, w in enumerate(entries):
                     inverse = lax.rsqrt(square[:, k * panels : (k + 1) * panels])
-                    running = running + inverse * weight_v[w]
+                    running = running + inverse * right_v[w, 7:8, :]
             total = jnp.sum(running, axis=1, keepdims=True)
             near_v[...] = jnp.where(pair_lane == t, total, near_v[...])
             return carry
 
-        lax.fori_loop(0, leaves, to_near, 0)
+        lax.fori_loop(0, leaves, to_near, 0, unroll=8)
         nearby = near_v[...].T[:leaves]
 
         image = (0.5 * current + nearby + distant) * mask
@@ -403,20 +452,22 @@
         in_specs=[vmem, vmem, vmem, smem, smem, vmem, vmem, anywhere, anywhere, anywhere],
         out_specs=(vmem, vmem),
         scratch_shapes=[
-            pltpu.VMEM((leaves, terms, panels), bf16),
-            pltpu.VMEM((leaves, panels, terms), bf16),
-            pltpu.VMEM((offsets, terms, terms), bf16),
+            pltpu.VMEM((terms, leaves, panels), bf16),
+            pltpu.VMEM((terms, leaves, panels), bf16),
+            pltpu.VMEM((terms, offsets, terms), bf16),
             pltpu.VMEM((slots, 5, leaves, panels), f32),
             pltpu.VMEM((slots, leaves, lanes), f32),
             pltpu.VMEM((leaves, far_pad), jnp.int32),
             pltpu.VMEM((leaves, far_pad), jnp.int32),
             pltpu.VMEM((leaves, off_pad, wide), bf16),
-            pltpu.VMEM((leaves * off_pad, lanes), f32),
+            pltpu.VMEM((leaves * off_step, lanes), f32),
             pltpu.VMEM((leaves, panels, lanes), bf16),
-            pltpu.VMEM((window, rows, panels), f32),
-            pltpu.VMEM((window, 1, panels), f32),
-            pltpu.VMEM((leaves * 2 * rows, panels), f32),
+            pltpu.VMEM((window, row_step, panels), f32),
+            pltpu.VMEM((leaves * part_step, panels), f32),
             pltpu.VMEM((panels, lanes), f32),
+            pltpu.VMEM((folded_rows, lanes), f32),
+            pltpu.VMEM((folded_rows, lanes), f32),
+            pltpu.VMEM((2, folded_rows, lanes), f32),
             pltpu.VMEM((group_a, krylov, lanes), f32),
             pltpu.VMEM((group_b, krylov, lanes), f32),
             dma((3,)),
@@ -446,7 +497,8 @@
             near_list.shape[1], far_list.shape[1],
         )
         vector, hessenberg = step(
-            basis, coords, areas, counts, near_list, far_list, far_offset, p2m, l2p, m2l
+            basis, coords.transpose(1, 0, 2), areas, counts, near_list, far_list, far_offset,
+            p2m.transpose(1, 0, 2), l2p.transpose(2, 0, 1), m2l.transpose(1, 0, 2),
         )
         return vector, hessenberg[0, : krylov + 1]
 

time: 93.6 us -> 51 us (0.54)
  Pallas kernels: 69.2 us -> 47 us
  local copies, waits for them, and re-layouts: 22.6 us -> 2.44 us
    pallas_call x1, Pallas kernels: 69.2 us -> 47 us  [on_device(): step(basis, coords.transpose(1, 0, 2), areas, counts, near_list, far_list...]
    unnamed x5 -> x1, local copies, waits for them, and re-layouts: 21.5 us -> 1.31 us
where the time goes in v2:
time: 51 us; the launch traced here: 50.8 us
  Pallas kernels  47 us (92%)
  local copies, waits for them, and re-layouts  2.44 us (5%)
  between operations  1.29 us (3%)
    pallas_call x1, Pallas kernels, on_device(): step(basis, coords.transpose(1, 0, 2), areas, counts, near_list, far_list...  47 us
    unnamed x1, local copies, waits for them, and re-layouts  1.31 us
    squeeze x1, local copies, waits for them, and re-layouts, on_device(): return (vector, hessenberg[0, :krylov + 1])  1.14 us

profile of v2, /device:TPU:1, one launch (start us, length us, event | category | flops | bytes accessed | tf_op | source)
XLA Modules:
  0.0 50.8 jit_solution(8253638506345866583)
XLA Ops:
  1.3 47.0 %shard_map.113 = (f32[24,128]{1,0:T(8,128)}, f32[1,128]{1,0:T(1,128)}) custom-call(f32[8,24,128]{2,1,0:T(8,128)} %basis_ref.1, f32[3,24,128]{2,1,0:T(8,128)} %bitcast.9, f32[24,128]{1,0:T(8,128)} %areas_ref.1, s32[1]{0:T(128)S(6)} %copy.13.counts_ref, s32[24,27]{1,0:T(8,128)} %near_ref.1, s32[24,189]{1,0:T(8,128)} %far_ref.1, s32[24,189]{1,0:T(8,128)} %off_ref.1, ...), custom_call_target="tpu_custom_call" | custom-call | tf_op jit(solution)/shard_map/pallas_call | solution.py:499
  48.3 1.1 %slice_bitcast_fusion = f32[9]{0:T(128)} fusion(f32[1,128]{1,0:T(1,128)} %get-tuple-element.5), kind=kLoop, calls=%fused_computation | loop fusion | bytes 72 | tf_op jit(solution)/shard_map/squeeze | solution.py:503
  49.5 1.3 %copy.14 = f32[24,128]{1,0:T(8,128)} copy(f32[24,128]{1,0:T(8,128)} %get-tuple-element.8) | data formatting | bytes 24576

commit v3 on v2

--- a/solution.py
+++ b/solution.py
@@ -38,7 +38,7 @@
     window = 3 * nx * leaves
     wide = round_up(window, 128)
     off_pad = round_up(offsets, 16)
-    off_step = off_pad + 8
+    off_step = off_pad + 4
     far_pad = round_up(far, 128)
     lanes = 128
     group_a = nx * nc
@@ -47,14 +47,16 @@
     row_step = 24
     part_step = 40
     group = 8
-    folded_rows = group * lanes
+    leaf_step = group + 1
+    folded_rows = round_up((lanes - 1) * leaf_step + group, 8)
+    buffers = 4
 
     def kernel(
         basis_ref, coords_ref, areas_ref, counts_ref, near_ref, far_ref, off_ref,
         p2m_hbm, l2p_hbm, m2l_hbm,
         vec_ref, hess_ref,
         p2m_v, l2p_v, m2l_v, panels_v, poles_v, far_v, off_v, count_v, sum_v, left_v,
-        right_v, part_v, near_v, p2m_f, l2p_f, m2l_f, stage_a, stage_b,
+        right_v, part_v, near_v, p2m_f, l2p_f, m2l_f, pair_v, stage_a, stage_b,
         load_sem, pole_send, pole_recv, panel_send, panel_recv, a_send, a_recv, b_send, b_recv,
     ):
         y, z, c, x = (lax.axis_index(name) for name in AXES)
@@ -106,16 +108,16 @@
         loads[0].wait()
 
         def unfold(source, scratch, part, count):
-            block = source[:, pl.ds(pl.multiple_of(part * group, group), count), :].astype(f32)
+            start = part * group
+            if not isinstance(part, int):
+                start = pl.multiple_of(start, group)
+            block = source[:, pl.ds(start, count), :].astype(f32)
             width = block.shape[2]
-            if count == group:
-                scratch[: block.shape[0] * group, :width] = block.reshape(-1, width)
-            else:
-                for k in range(block.shape[0]):
-                    scratch[k * group : k * group + count, :width] = block[k]
+            for k in range(block.shape[0]):
+                scratch[k * leaf_step : k * leaf_step + count, :width] = block[k]
 
         def unfolded(scratch, k):
-            return scratch[pl.ds(k, lanes, stride=group), :].astype(bf16)
+            return scratch[pl.ds(k, lanes, stride=leaf_step), :].astype(bf16)
 
         def per_leaf(values, source, scratch, dims, running):
             def one_group(part, running):
@@ -139,53 +141,6 @@
         right_v[:, :rows, :] = pattern
         for scratch in (l2p_f, m2l_f):
             scratch[...] = jnp.zeros(scratch.shape, f32)
-
-        pl.semaphore_wait(barrier, len(everyone))
-
-        def send(buffer, sends, recvs, number, source, target_slot, peer):
-            copy = pltpu.make_async_remote_copy(
-                src_ref=buffer.at[source],
-                dst_ref=buffer.at[target_slot],
-                send_sem=sends.at[number],
-                recv_sem=recvs.at[target_slot],
-                device_id=peer,
-                device_id_type=MESH,
-            )
-            copy.start()
-            return copy
-
-        sent = []
-
-        def first_sends(buffer, sends, recvs):
-            for r in range(1, nx):
-                sent.append(send(buffer, sends, recvs, r - 1, own, own, (y, z, c, ring(r))))
-            base = nx - 1
-            sent.append(send(buffer, sends, recvs, base, own, 2 * nx * c + x, partner))
-            sent.append(send(buffer, sends, recvs, base + 1, own, 2 * nx * (1 - c) + x, across))
-
-        def received(buffer, sends, recvs, slot):
-            pltpu.make_async_remote_copy(
-                src_ref=buffer.at[slot],
-                dst_ref=buffer.at[slot],
-                send_sem=sends.at[0],
-                recv_sem=recvs.at[slot],
-                device_id=partner,
-                device_id_type=MESH,
-            ).wait_recv()
-
-        def forward(buffer, sends, recvs, r):
-            other = ring(r)
-            received(buffer, sends, recvs, nx + other)
-            base = nx + 1 + 2 * (r - 1)
-            sent.append(send(buffer, sends, recvs, base, nx + other, 2 * nx * c + other, partner))
-            sent.append(
-                send(buffer, sends, recvs, base + 1, nx + other, 2 * nx * (1 - c) + other, across)
-            )
-
-        pole_set = (poles_v, pole_send, pole_recv)
-        panel_set = (panels_v, panel_send, panel_recv)
-        first_sends(*pole_set)
-        first_sends(*panel_set)
 
         far_v[...] = jnp.full(far_v.shape, -1, jnp.int32)
         off_v[...] = jnp.full(off_v.shape, -1, jnp.int32)
@@ -206,15 +161,7 @@
             count_v[t] = pairs.astype(bf16)
             return carry
 
-        third = leaves // 4
-        lax.fori_loop(0, 2 * third, to_counts, 0, unroll=2)
-        forward(*pole_set, 1)
-        forward(*pole_set, nx - 1)
-        lax.fori_loop(2 * third, 3 * third, to_counts, 0, unroll=2)
-        forward(*pole_set, nx // 2)
-        forward(*panel_set, 1)
-        forward(*panel_set, nx - 1)
-        lax.fori_loop(3 * third, leaves, to_counts, 0, unroll=2)
+        lax.fori_loop(0, leaves, to_counts, 0, unroll=4)
 
         left_v[...] = jnp.zeros(left_v.shape, bf16)
         own_comps = [panels_v[own, comp] - 2.0 for comp in range(3)]
@@ -238,8 +185,6 @@
             return carry
 
         lax.fori_loop(0, leaves, to_left, 0, unroll=4)
-        forward(*panel_set, nx // 2)
-
         tile_lane = lax.broadcasted_iota(jnp.int32, (krylov, lanes), 1)
         masked = [basis_ref[j] * mask for j in range(krylov)]
 
@@ -259,6 +204,81 @@
         for j in range(krylov):
             tile = jnp.where(tile_lane == j, inner_products(masked[j]), tile)
         tile = jnp.where(tile_lane == krylov + 2, full_sum(folded(mask)), tile)
+
+        pl.semaphore_wait(barrier, len(everyone))
+
+        def send(buffer, sends, recvs, number, source, target_slot, peer):
+            copy = pltpu.make_async_remote_copy(
+                src_ref=buffer.at[source],
+                dst_ref=buffer.at[target_slot],
+                send_sem=sends.at[number],
+                recv_sem=recvs.at[target_slot],
+                device_id=peer,
+                device_id_type=MESH,
+            )
+            copy.start()
+            return copy
+
+        sent = []
+
+        def first_sends(buffer, sends, recvs):
+            for r in range(1, nx):
+                sent.append(send(buffer, sends, recvs, r - 1, own, own, (y, z, c, ring(r))))
+            base = nx - 1
+            sent.append(send(buffer, sends, recvs, base, own, 2 * nx * c + x, partner))
+            sent.append(send(buffer, sends, recvs, base + 1, own, 2 * nx * (1 - c) + x, across))
+
+        def received(buffer, sends, recvs, slot):
+            pltpu.make_async_remote_copy(
+                src_ref=buffer.at[slot],
+                dst_ref=buffer.at[slot],
+                send_sem=sends.at[0],
+                recv_sem=recvs.at[slot],
+                device_id=partner,
+                device_id_type=MESH,
+            ).wait_recv()
+
+        def forward(buffer, sends, recvs, r):
+            other = ring(r)
+            received(buffer, sends, recvs, nx + other)
+            base = nx + 1 + 2 * (r - 1)
+            sent.append(send(buffer, sends, recvs, base, nx + other, 2 * nx * c + other, partner))
+            sent.append(
+                send(buffer, sends, recvs, base + 1, nx + other, 2 * nx * (1 - c) + other, across)
+            )
+
+        pole_set = (poles_v, pole_send, pole_recv)
+        panel_set = (panels_v, panel_send, panel_recv)
+        first_sends(*pole_set)
+        first_sends(*panel_set)
+
+        loads[1].wait()
+
+        def set_apart(part, buffer, count):
+            scratch = m2l_f.at[buffer]
+            unfold(m2l_v, scratch, part, count)
+            for k in range(count):
+                pair_v[part * group + k] = unfolded(scratch, k)
+
+        def set_apart_all(step, carry):
+            for buffer in range(buffers):
+                set_apart(buffers * step + buffer, buffer, group)
+            return carry
+
+        whole = offsets // group
+        steps = whole // buffers
+        lax.fori_loop(0, steps // 2, set_apart_all, 0)
+        forward(*pole_set, 1)
+        forward(*pole_set, nx - 1)
+        lax.fori_loop(steps // 2, steps, set_apart_all, 0)
+        for part in range(steps * buffers, whole):
+            set_apart(part, part % buffers, group)
+        if offsets % group:
+            set_apart(whole, whole % buffers, offsets % group)
+        forward(*pole_set, nx // 2)
+        forward(*panel_set, 1)
+        forward(*panel_set, nx - 1)
+        forward(*panel_set, nx // 2)
 
         valid_before = (seg > 0).astype(f32)
         valid_after = (seg < segments - 1).astype(f32)
@@ -285,43 +305,28 @@
 
         def to_sums(t, carry):
             both = jnp.dot(count_v[t], both_poles, preferred_element_type=f32)
-            start = pl.multiple_of(t * off_step, 8)
-            sum_v[pl.ds(start, off_pad), :] = both[:, :lanes] + both[:, lanes:]
+            sum_v[pl.ds(t * off_step, off_pad), :] = both[:, :lanes] + both[:, lanes:]
             return carry
 
-        lax.fori_loop(0, leaves, to_sums, 0, unroll=2)
-
-        loads[1].wait()
-
-        def add_local(part, half, count, running):
-            scratch = m2l_f.at[half]
-            unfold(m2l_v, scratch, part, count)
-            for k in range(0, count, 2):
-                lefts, rights = [], []
-                for o in (k, k + 1):
-                    sums = sum_v[pl.ds(part * group + o, leaves, stride=off_step), :]
-                    high, low = high_low(sums)
-                    lefts.append(jnp.concatenate([high, low], axis=0).astype(bf16))
-                    rights.append(unfolded(scratch, o))
-                running = running + lax.dot_general(
-                    jnp.concatenate(lefts, axis=1),
-                    jnp.concatenate(rights, axis=1),
-                    NT,
-                    preferred_element_type=f32,
-                )
-            return running
-
-        def to_local(step, running):
-            for half in range(2):
-                running = add_local(2 * step + half, half, group, running)
-            return running
-
-        whole = offsets // group
-        both = lax.fori_loop(0, whole // 2, to_local, jnp.zeros((2 * leaves, lanes), f32))
-        for part in range(whole // 2 * 2, whole):
-            both = add_local(part, 0, group, both)
-        if offsets % group:
-            both = add_local(whole, 1, offsets % group, both)
+        lax.fori_loop(0, leaves, to_sums, 0, unroll=6)
+
+        def to_local(pair, running):
+            lefts, rights = [], []
+            for o in range(2):
+                sums = sum_v[pl.ds(2 * pair + o, leaves, stride=off_step), :]
+                high, low = high_low(sums)
+                lefts.append(jnp.concatenate([high, low], axis=0).astype(bf16))
+                rights.append(pair_v[2 * pair + o])
+            return running + lax.dot_general(
+                jnp.concatenate(lefts, axis=1),
+                jnp.concatenate(rights, axis=1),
+                NT,
+                preferred_element_type=f32,
+            )
+
+        both = lax.fori_loop(
+            0, offsets // 2, to_local, jnp.zeros((2 * leaves, lanes), f32), unroll=40
+        )
         inside = lax.broadcasted_iota(jnp.int32, (leaves, lanes), 1) < terms
         local = tall(jnp.where(inside, both[:leaves] + both[leaves:], 0.0))
         loads[2].wait()
@@ -467,7 +472,8 @@
             pltpu.VMEM((panels, lanes), f32),
             pltpu.VMEM((folded_rows, lanes), f32),
             pltpu.VMEM((folded_rows, lanes), f32),
-            pltpu.VMEM((2, folded_rows, lanes), f32),
+            pltpu.VMEM((buffers, folded_rows, lanes), f32),
+            pltpu.VMEM((offsets, lanes, lanes), bf16),
             pltpu.VMEM((group_a, krylov, lanes), f32),
             pltpu.VMEM((group_b, krylov, lanes), f32),
             dma((3,)),

time: 51 us -> 52.9 us (1.037)
  Pallas kernels: 47 us -> 48.7 us
    pallas_call x1, Pallas kernels: 47 us -> 48.7 us  [on_device(): step(basis, coords.transpose(1, 0, 2), areas, counts, near_list, far_list...]
where the time goes in v3:
time: 52.9 us; the launch traced here: 52.4 us
  Pallas kernels  48.7 us (92%)
  local copies, waits for them, and re-layouts  2.44 us (5%)
  between operations  1.29 us (2%)
    pallas_call x1, Pallas kernels, on_device(): step(basis, coords.transpose(1, 0, 2), areas, counts, near_list, far_list...  48.7 us
    unnamed x1, local copies, waits for them, and re-layouts  1.31 us
    squeeze x1, local copies, waits for them, and re-layouts, on_device(): return (vector, hessenberg[0, :krylov + 1])  1.14 us

profile of v3, /device:TPU:1, one launch (start us, length us, event | category | flops | bytes accessed | tf_op | source)
XLA Modules:
  0.0 52.4 jit_solution(10362047238500410793)
XLA Ops:
  1.3 48.7 %shard_map.113 = (f32[24,128]{1,0:T(8,128)}, f32[1,128]{1,0:T(1,128)}) custom-call(f32[8,24,128]{2,1,0:T(8,128)} %basis_ref.1, f32[3,24,128]{2,1,0:T(8,128)} %bitcast.9, f32[24,128]{1,0:T(8,128)} %areas_ref.1, s32[1]{0:T(128)S(6)} %copy.13.counts_ref, s32[24,27]{1,0:T(8,128)} %near_ref.1, s32[24,189]{1,0:T(8,128)} %far_ref.1, s32[24,189]{1,0:T(8,128)} %off_ref.1, ...), custom_call_target="tpu_custom_call" | custom-call | tf_op jit(solution)/shard_map/pallas_call | solution.py:505
  50.0 1.1 %slice_bitcast_fusion = f32[9]{0:T(128)} fusion(f32[1,128]{1,0:T(1,128)} %get-tuple-element.5), kind=kLoop, calls=%fused_computation | loop fusion | bytes 72 | tf_op jit(solution)/shard_map/squeeze | solution.py:509
  51.1 1.3 %copy.14 = f32[24,128]{1,0:T(8,128)} copy(f32[24,128]{1,0:T(8,128)} %get-tuple-element.8) | data formatting | bytes 24576

commit v4 on v3

--- a/solution.py
+++ b/solution.py
@@ -60,6 +60,9 @@
         load_sem, pole_send, pole_recv, panel_send, panel_recv, a_send, a_recv, b_send, b_recv,
     ):
         y, z, c, x = (lax.axis_index(name) for name in AXES)
+        ys = [y] + [lax.rem(y + k, ny) for k in range(1, ny)]
+        zs = [z] + [lax.rem(z + k, nz) for k in range(1, nz)]
+        xs = [x] + [lax.rem(x + k, nx) for k in range(1, nx)]
         q = y * nz + z
         seg = q * nc + c
         q_across = lax.rem(q + group_b - 1 + 2 * c, group_b)
@@ -72,20 +75,16 @@
         for load in loads:
             load.start()
 
-        def ring(step):
-            return lax.rem(x + step, nx)
-
         partner = (y, z, 1 - c, x)
         across = (y_across, z_across, 1 - c, x)
-        peers_a = [(y, z, c, ring(r)) for r in range(1, nx)]
-        peers_a += [(y, z, 1 - c, ring(r)) for r in range(nx)]
-        peers_b = []
-        for r in range(1, group_b):
-            other = lax.rem(q + r, group_b)
-            peers_b.append((other // nz, lax.rem(other, nz), c, x))
+        row_own = [(y, z, c, other) for other in xs]
+        row_partner = [(y, z, 1 - c, other) for other in xs]
+        row_across = [(y_across, z_across, 1 - c, other) for other in xs]
+        peers_b = [(other_y, other_z, c, x) for other_y in ys for other_z in zs][1:]
+        slots_b = [other_y * nz + other_z for other_y in ys for other_z in zs][1:]
 
         barrier = pltpu.get_barrier_semaphore()
-        everyone = peers_a + peers_b + [across]
+        everyone = row_own[1:] + row_partner + row_across + peers_b
         for peer in everyone:
             pl.semaphore_signal(barrier, inc=1, device_id=peer, device_id_type=MESH)
 
@@ -205,6 +204,26 @@
             tile = jnp.where(tile_lane == j, inner_products(masked[j]), tile)
         tile = jnp.where(tile_lane == krylov + 2, full_sum(folded(mask)), tile)
 
+        loads[1].wait()
+
+        def set_apart(part, buffer, count):
+            scratch = m2l_f.at[buffer]
+            unfold(m2l_v, scratch, part, count)
+            for k in range(count):
+                pair_v[part * group + k] = unfolded(scratch, k)
+
+        def set_apart_all(step, carry):
+            for buffer in range(buffers):
+                set_apart(buffers * step + buffer, buffer, group)
+            return carry
+
+        whole = offsets // group
+        steps = whole // buffers
+        lax.fori_loop(0, steps, set_apart_all, 0)
+        for part in range(steps * buffers, whole):
+            set_apart(part, part % buffers, group)
+        if offsets % group:
+            set_apart(whole, whole % buffers, offsets % group)
         pl.semaphore_wait(barrier, len(everyone))
 
         def send(buffer, sends, recvs, number, source, target_slot, peer):
@@ -221,12 +240,23 @@
 
         sent = []
 
-        def first_sends(buffer, sends, recvs):
-            for r in range(1, nx):
-                sent.append(send(buffer, sends, recvs, r - 1, own, own, (y, z, c, ring(r))))
-            base = nx - 1
-            sent.append(send(buffer, sends, recvs, base, own, 2 * nx * c + x, partner))
-            sent.append(send(buffer, sends, recvs, base + 1, own, 2 * nx * (1 - c) + x, across))
+        slot_partner = 2 * nx * c
+        slot_across = 2 * nx * (1 - c)
+
+        def pole_sends():
+            for k in range(nx):
+                buffers = (poles_v, pole_send, pole_recv)
+                if k:
+                    sent.append(send(*buffers, k - 1, own, own, row_own[k]))
+                sent.append(send(*buffers, nx - 1 + k, own, slot_partner + x, row_partner[k]))
+                sent.append(send(*buffers, 2 * nx - 1 + k, own, slot_across + x, row_across[k]))
+
+        def panel_sends():
+            buffers = (panels_v, panel_send, panel_recv)
+            for k in range(1, nx):
+                sent.append(send(*buffers, k - 1, own, own, row_own[k]))
+            sent.append(send(*buffers, nx - 1, own, slot_partner + x, partner))
+            sent.append(send(*buffers, nx, own, slot_across + x, across))
 
         def received(buffer, sends, recvs, slot):
             pltpu.make_async_remote_copy(
@@ -238,47 +268,17 @@
                 device_id_type=MESH,
             ).wait_recv()
 
-        def forward(buffer, sends, recvs, r):
-            other = ring(r)
-            received(buffer, sends, recvs, nx + other)
+        def forward(r):
+            buffers = (panels_v, panel_send, panel_recv)
+            received(*buffers, nx + xs[r])
             base = nx + 1 + 2 * (r - 1)
-            sent.append(send(buffer, sends, recvs, base, nx + other, 2 * nx * c + other, partner))
-            sent.append(
-                send(buffer, sends, recvs, base + 1, nx + other, 2 * nx * (1 - c) + other, across)
-            )
+            sent.append(send(*buffers, base, nx + xs[r], slot_partner + xs[r], partner))
+            sent.append(send(*buffers, base + 1, nx + xs[r], slot_across + xs[r], across))
 
         pole_set = (poles_v, pole_send, pole_recv)
         panel_set = (panels_v, panel_send, panel_recv)
-        first_sends(*pole_set)
-        first_sends(*panel_set)
-
-        loads[1].wait()
-
-        def set_apart(part, buffer, count):
-            scratch = m2l_f.at[buffer]
-            unfold(m2l_v, scratch, part, count)
-            for k in range(count):
-                pair_v[part * group + k] = unfolded(scratch, k)
-
-        def set_apart_all(step, carry):
-            for buffer in range(buffers):
-                set_apart(buffers * step + buffer, buffer, group)
-            return carry
-
-        whole = offsets // group
-        steps = whole // buffers
-        lax.fori_loop(0, steps // 2, set_apart_all, 0)
-        forward(*pole_set, 1)
-        forward(*pole_set, nx - 1)
-        lax.fori_loop(steps // 2, steps, set_apart_all, 0)
-        for part in range(steps * buffers, whole):
-            set_apart(part, part % buffers, group)
-        if offsets % group:
-            set_apart(whole, whole % buffers, offsets % group)
-        forward(*pole_set, nx // 2)
-        forward(*panel_set, 1)
-        forward(*panel_set, nx - 1)
-        forward(*panel_set, nx // 2)
+        pole_sends()
+        panel_sends()
 
         valid_before = (seg > 0).astype(f32)
         valid_after = (seg < segments - 1).astype(f32)
@@ -288,6 +288,8 @@
                 recv(k)
                 recv(2 * nx + k)
 
+        for r in range(1, nx):
+            received(*pole_set, nx + xs[r])
         outside_slots(lambda slot: received(*pole_set, slot))
 
         pole_parts = []
@@ -308,25 +310,27 @@
             sum_v[pl.ds(t * off_step, off_pad), :] = both[:, :lanes] + both[:, lanes:]
             return carry
 
-        lax.fori_loop(0, leaves, to_sums, 0, unroll=6)
-
-        def to_local(pair, running):
+        lax.fori_loop(0, leaves // 2, to_sums, 0, unroll=6)
+        forward(1)
+        forward(nx - 1)
+        lax.fori_loop(leaves // 2, leaves, to_sums, 0, unroll=6)
+        forward(nx // 2)
+
+        def to_local(first, count):
             lefts, rights = [], []
-            for o in range(2):
-                sums = sum_v[pl.ds(2 * pair + o, leaves, stride=off_step), :]
-                high, low = high_low(sums)
+            for o in range(first, first + count):
+                high, low = high_low(sum_v[pl.ds(o, leaves, stride=off_step), :])
                 lefts.append(jnp.concatenate([high, low], axis=0).astype(bf16))
-                rights.append(pair_v[2 * pair + o])
-            return running + lax.dot_general(
+                rights.append(pair_v[o])
+            return lax.dot_general(
                 jnp.concatenate(lefts, axis=1),
                 jnp.concatenate(rights, axis=1),
                 NT,
                 preferred_element_type=f32,
             )
 
-        both = lax.fori_loop(
-            0, offsets // 2, to_local, jnp.zeros((2 * leaves, lanes), f32), unroll=40
-        )
+        half = round_up(offsets // 2, 2)
+        both = to_local(0, half) + to_local(half, offsets - half)
         inside = lax.broadcasted_iota(jnp.int32, (leaves, lanes), 1) < terms
         local = tall(jnp.where(inside, both[:leaves] + both[leaves:], 0.0))
         loads[2].wait()
@@ -411,10 +415,10 @@
             sent.extend(copies)
             return total
 
-        others_a = [(ring(r) * nc + c, (y, z, c, ring(r))) for r in range(1, nx)]
-        others_a += [(ring(r) * nc + 1 - c, (y, z, 1 - c, ring(r))) for r in range(nx)]
+        others_a = [(xs[r] * nc + c, row_own[r]) for r in range(1, nx)]
+        others_a += [(xs[r] * nc + 1 - c, row_partner[r]) for r in range(nx)]
         tile = exchange(stage_a, a_send, a_recv, x * nc + c, others_a, tile)
-        others_b = [(lax.rem(q + r, group_b), peers_b[r - 1]) for r in range(1, group_b)]
+        others_b = list(zip(slots_b, peers_b))
         tile = exchange(stage_b, b_send, b_recv, q, others_b, tile)
 
         def column(index):
@@ -447,7 +451,7 @@
     anywhere = pl.BlockSpec(memory_space=pl.ANY)
     dma = pltpu.SemaphoreType.DMA
     slots = 3 * nx
-    n_sends = nx + 1 + 2 * (nx - 1)
+    n_sends = 3 * nx
     return pl.pallas_call(
         kernel,
         out_shape=(

time: 52.9 us -> 48.6 us (0.919)
  Pallas kernels: 48.7 us -> 44.6 us
    pallas_call x1, Pallas kernels: 48.7 us -> 44.6 us  [on_device(): step(basis, coords.transpose(1, 0, 2), areas, counts, near_list, far_list...]
where the time goes in v4:
time: 48.6 us; the launch traced here: 48.4 us
  Pallas kernels  44.6 us (92%)
  local copies, waits for them, and re-layouts  2.44 us (5%)
  between operations  1.29 us (3%)
    pallas_call x1, Pallas kernels, on_device(): step(basis, coords.transpose(1, 0, 2), areas, counts, near_list, far_list...  44.6 us
    unnamed x1, local copies, waits for them, and re-layouts  1.31 us
    squeeze x1, local copies, waits for them, and re-layouts, on_device(): return (vector, hessenberg[0, :krylov + 1])  1.14 us

profile of v4, /device:TPU:1, one launch (start us, length us, event | category | flops | bytes accessed | tf_op | source)
XLA Modules:
  0.0 48.4 jit_solution(10870891795332906012)
XLA Ops:
  1.3 44.6 %shard_map.113 = (f32[24,128]{1,0:T(8,128)}, f32[1,128]{1,0:T(1,128)}) custom-call(f32[8,24,128]{2,1,0:T(8,128)} %basis_ref.1, f32[3,24,128]{2,1,0:T(8,128)} %bitcast.9, f32[24,128]{1,0:T(8,128)} %areas_ref.1, s32[1]{0:T(128)S(6)} %copy.13.counts_ref, s32[24,27]{1,0:T(8,128)} %near_ref.1, s32[24,189]{1,0:T(8,128)} %far_ref.1, s32[24,189]{1,0:T(8,128)} %off_ref.1, ...), custom_call_target="tpu_custom_call" | custom-call | tf_op jit(solution)/shard_map/pallas_call | solution.py:509
  45.9 1.1 %slice_bitcast_fusion = f32[9]{0:T(128)} fusion(f32[1,128]{1,0:T(1,128)} %get-tuple-element.5), kind=kLoop, calls=%fused_computation | loop fusion | bytes 72 | tf_op jit(solution)/shard_map/squeeze | solution.py:513
  47.1 1.3 %copy.14 = f32[24,128]{1,0:T(8,128)} copy(f32[24,128]{1,0:T(8,128)} %get-tuple-element.8) | data formatting | bytes 24576

commit v5 on v4

--- a/solution.py
+++ b/solution.py
@@ -136,6 +136,62 @@
         poles_v[own] = jnp.zeros((leaves, lanes), f32)
         poles_v[own, :, :terms] = multipoles[:leaves, :terms]
 
+        pl.semaphore_wait(barrier, len(everyone))
+
+        def send(buffer, sends, recvs, number, source, target_slot, peer):
+            copy = pltpu.make_async_remote_copy(
+                src_ref=buffer.at[source],
+                dst_ref=buffer.at[target_slot],
+                send_sem=sends.at[number],
+                recv_sem=recvs.at[target_slot],
+                device_id=peer,
+                device_id_type=MESH,
+            )
+            copy.start()
+            return copy
+
+        sent = []
+
+        slot_partner = 2 * nx * c
+        slot_across = 2 * nx * (1 - c)
+
+        def pole_sends():
+            for k in range(nx):
+                buffers = (poles_v, pole_send, pole_recv)
+                if k:
+                    sent.append(send(*buffers, k - 1, own, own, row_own[k]))
+                sent.append(send(*buffers, nx - 1 + k, own, slot_partner + x, row_partner[k]))
+                sent.append(send(*buffers, 2 * nx - 1 + k, own, slot_across + x, row_across[k]))
+
+        def panel_sends():
+            buffers = (panels_v, panel_send, panel_recv)
+            for k in range(1, nx):
+                sent.append(send(*buffers, k - 1, own, own, row_own[k]))
+            sent.append(send(*buffers, nx - 1, own, slot_partner + x, partner))
+            sent.append(send(*buffers, nx, own, slot_across + x, across))
+
+        def received(buffer, sends, recvs, slot):
+            pltpu.make_async_remote_copy(
+                src_ref=buffer.at[slot],
+                dst_ref=buffer.at[slot],
+                send_sem=sends.at[0],
+                recv_sem=recvs.at[slot],
+                device_id=partner,
+                device_id_type=MESH,
+            ).wait_recv()
+
+        def forward(r):
+            buffers = (panels_v, panel_send, panel_recv)
+            received(*buffers, nx + xs[r])
+            base = nx + 1 + 2 * (r - 1)
+            sent.append(send(*buffers, base, nx + xs[r], slot_partner + xs[r], partner))
+            sent.append(send(*buffers, base + 1, nx + xs[r], slot_across + xs[r], across))
+
+        pole_set = (poles_v, pole_send, pole_recv)
+        panel_set = (panels_v, panel_send, panel_recv)
+        pole_sends()
+        panel_sends()
+
         pattern = (lax.broadcasted_iota(jnp.int32, (window, rows, panels), 1) == 6).astype(f32)
         right_v[:, :rows, :] = pattern
         for scratch in (l2p_f, m2l_f):
@@ -204,6 +260,8 @@
             tile = jnp.where(tile_lane == j, inner_products(masked[j]), tile)
         tile = jnp.where(tile_lane == krylov + 2, full_sum(folded(mask)), tile)
 
+        forward(1)
+        forward(nx - 1)
         loads[1].wait()
 
         def set_apart(part, buffer, count):
@@ -219,66 +277,13 @@
 
         whole = offsets // group
         steps = whole // buffers
-        lax.fori_loop(0, steps, set_apart_all, 0)
+        lax.fori_loop(0, steps // 2, set_apart_all, 0)
+        forward(nx // 2)
+        lax.fori_loop(steps // 2, steps, set_apart_all, 0)
         for part in range(steps * buffers, whole):
             set_apart(part, part % buffers, group)
         if offsets % group:
             set_apart(whole, whole % buffers, offsets % group)
-        pl.semaphore_wait(barrier, len(everyone))
-
-        def send(buffer, sends, recvs, number, source, target_slot, peer):
-            copy = pltpu.make_async_remote_copy(
-                src_ref=buffer.at[source],
-                dst_ref=buffer.at[target_slot],
-                send_sem=sends.at[number],
-                recv_sem=recvs.at[target_slot],
-                device_id=peer,
-                device_id_type=MESH,
-            )
-            copy.start()
-            return copy
-
-        sent = []
-
-        slot_partner = 2 * nx * c
-        slot_across = 2 * nx * (1 - c)
-
-        def pole_sends():
-            for k in range(nx):
-                buffers = (poles_v, pole_send, pole_recv)
-                if k:
-                    sent.append(send(*buffers, k - 1, own, own, row_own[k]))
-                sent.append(send(*buffers, nx - 1 + k, own, slot_partner + x, row_partner[k]))
-                sent.append(send(*buffers, 2 * nx - 1 + k, own, slot_across + x, row_across[k]))
-
-        def panel_sends():
-            buffers = (panels_v, panel_send, panel_recv)
-            for k in range(1, nx):
-                sent.append(send(*buffers, k - 1, own, own, row_own[k]))
-            sent.append(send(*buffers, nx - 1, own, slot_partner + x, partner))
-            sent.append(send(*buffers, nx, own, slot_across + x, across))
-
-        def received(buffer, sends, recvs, slot):
-            pltpu.make_async_remote_copy(
-                src_ref=buffer.at[slot],
-                dst_ref=buffer.at[slot],
-                send_sem=sends.at[0],
-                recv_sem=recvs.at[slot],
-                device_id=partner,
-                device_id_type=MESH,
-            ).wait_recv()
-
-        def forward(r):
-            buffers = (panels_v, panel_send, panel_recv)
-            received(*buffers, nx + xs[r])
-            base = nx + 1 + 2 * (r - 1)
-            sent.append(send(*buffers, base, nx + xs[r], slot_partner + xs[r], partner))
-            sent.append(send(*buffers, base + 1, nx + xs[r], slot_across + xs[r], across))
-
-        pole_set = (poles_v, pole_send, pole_recv)
-        panel_set = (panels_v, panel_send, panel_recv)
-        pole_sends()
-        panel_sends()
 
         valid_before = (seg > 0).astype(f32)
         valid_after = (seg < segments - 1).astype(f32)
@@ -310,11 +315,7 @@
             sum_v[pl.ds(t * off_step, off_pad), :] = both[:, :lanes] + both[:, lanes:]
             return carry
 
-        lax.fori_loop(0, leaves // 2, to_sums, 0, unroll=6)
-        forward(1)
-        forward(nx - 1)
-        lax.fori_loop(leaves // 2, leaves, to_sums, 0, unroll=6)
-        forward(nx // 2)
+        lax.fori_loop(0, leaves, to_sums, 0, unroll=6)
 
         def to_local(first, count):
             lefts, rights = [], []

time: 48.6 us -> 46.6 us (0.959)
  Pallas kernels: 44.6 us -> 42.6 us
    pallas_call x1, Pallas kernels: 44.6 us -> 42.6 us  [on_device(): step(basis, coords.transpose(1, 0, 2), areas, counts, near_list, far_list...]
where the time goes in v5:
time: 46.6 us; the launch traced here: 46.3 us
  Pallas kernels  42.6 us (91%)
  local copies, waits for them, and re-layouts  2.44 us (5%)
  between operations  1.29 us (3%)
    pallas_call x1, Pallas kernels, on_device(): step(basis, coords.transpose(1, 0, 2), areas, counts, near_list, far_list...  42.6 us
    unnamed x1, local copies, waits for them, and re-layouts  1.31 us
    squeeze x1, local copies, waits for them, and re-layouts, on_device(): return (vector, hessenberg[0, :krylov + 1])  1.14 us

profile of v5, /device:TPU:1, one launch (start us, length us, event | category | flops | bytes accessed | tf_op | source)
XLA Modules:
  0.0 46.3 jit_solution(3158251135181490520)
XLA Ops:
  1.3 42.6 %shard_map.113 = (f32[24,128]{1,0:T(8,128)}, f32[1,128]{1,0:T(1,128)}) custom-call(f32[8,24,128]{2,1,0:T(8,128)} %basis_ref.1, f32[3,24,128]{2,1,0:T(8,128)} %bitcast.9, f32[24,128]{1,0:T(8,128)} %areas_ref.1, s32[1]{0:T(128)S(6)} %copy.13.counts_ref, s32[24,27]{1,0:T(8,128)} %near_ref.1, s32[24,189]{1,0:T(8,128)} %far_ref.1, s32[24,189]{1,0:T(8,128)} %off_ref.1, ...), custom_call_target="tpu_custom_call" | custom-call | tf_op jit(solution)/shard_map/pallas_call | solution.py:510
  43.9 1.1 %slice_bitcast_fusion = f32[9]{0:T(128)} fusion(f32[1,128]{1,0:T(1,128)} %get-tuple-element.5), kind=kLoop, calls=%fused_computation | loop fusion | bytes 72 | tf_op jit(solution)/shard_map/squeeze | solution.py:514
  45.0 1.3 %copy.14 = f32[24,128]{1,0:T(8,128)} copy(f32[24,128]{1,0:T(8,128)} %get-tuple-element.8) | data formatting | bytes 24576

commit v6 on v5

--- a/solution.py
+++ b/solution.py
@@ -12,6 +12,7 @@
 AXES = (Y, Z, C, X)
 MESH = pl.DeviceIdType.MESH
 NT = (((1,), (1,)), ((), ()))
+NN = (((1,), (0,)), ((), ()))
 four_pi = 12.566370614359172
 epsilon = 1e-06
 f32 = jnp.float32
@@ -268,7 +269,7 @@
             scratch = m2l_f.at[buffer]
             unfold(m2l_v, scratch, part, count)
             for k in range(count):
-                pair_v[part * group + k] = unfolded(scratch, k)
+                pair_v[part * group + k] = unfolded(scratch, k).T
 
         def set_apart_all(step, carry):
             for buffer in range(buffers):
@@ -325,8 +326,8 @@
                 rights.append(pair_v[o])
             return lax.dot_general(
                 jnp.concatenate(lefts, axis=1),
-                jnp.concatenate(rights, axis=1),
-                NT,
+                jnp.concatenate(rights, axis=0),
+                NN,
                 preferred_element_type=f32,
             )
 
@@ -335,8 +336,7 @@
         inside = lax.broadcasted_iota(jnp.int32, (leaves, lanes), 1) < terms
         local = tall(jnp.where(inside, both[:leaves] + both[leaves:], 0.0))
         loads[2].wait()
-        plain = (((1,), (0,)), ((), ()))
-        distant = per_leaf(local, l2p_v, l2p_f, plain, blank)[:leaves]
+        distant = per_leaf(local, l2p_v, l2p_f, NN, blank)[:leaves]
 
         outside_slots(lambda slot: received(*panel_set, slot))
 

time: 46.6 us -> 45.8 us (0.983)
  Pallas kernels: 42.6 us -> 41.8 us
    pallas_call x1, Pallas kernels: 42.6 us -> 41.8 us  [on_device(): step(basis, coords.transpose(1, 0, 2), areas, counts, near_list, far_list...]
where the time goes in v6:
time: 45.8 us; the launch traced here: 45.6 us
  Pallas kernels  41.8 us (91%)
  local copies, waits for them, and re-layouts  2.44 us (5%)
  between operations  1.29 us (3%)
    pallas_call x1, Pallas kernels, on_device(): step(basis, coords.transpose(1, 0, 2), areas, counts, near_list, far_list...  41.8 us
    unnamed x1, local copies, waits for them, and re-layouts  1.31 us
    squeeze x1, local copies, waits for them, and re-layouts, on_device(): return (vector, hessenberg[0, :krylov + 1])  1.14 us

profile of v6, /device:TPU:1, one launch (start us, length us, event | category | flops | bytes accessed | tf_op | source)
XLA Modules:
  0.0 45.6 jit_solution(9991859763806049502)
XLA Ops:
  1.3 41.8 %shard_map.113 = (f32[24,128]{1,0:T(8,128)}, f32[1,128]{1,0:T(1,128)}) custom-call(f32[8,24,128]{2,1,0:T(8,128)} %basis_ref.1, f32[3,24,128]{2,1,0:T(8,128)} %bitcast.9, f32[24,128]{1,0:T(8,128)} %areas_ref.1, s32[1]{0:T(128)S(6)} %copy.13.counts_ref, s32[24,27]{1,0:T(8,128)} %near_ref.1, s32[24,189]{1,0:T(8,128)} %far_ref.1, s32[24,189]{1,0:T(8,128)} %off_ref.1, ...), custom_call_target="tpu_custom_call" | custom-call | tf_op jit(solution)/shard_map/pallas_call | solution.py:510
  43.1 1.1 %slice_bitcast_fusion = f32[9]{0:T(128)} fusion(f32[1,128]{1,0:T(1,128)} %get-tuple-element.5), kind=kLoop, calls=%fused_computation | loop fusion | bytes 72 | tf_op jit(solution)/shard_map/squeeze | solution.py:514
  44.3 1.3 %copy.14 = f32[24,128]{1,0:T(8,128)} copy(f32[24,128]{1,0:T(8,128)} %get-tuple-element.8) | data formatting | bytes 24576

commit v7 on v6

--- a/solution.py
+++ b/solution.py
@@ -98,44 +98,11 @@
         panels_v[own, 3] = areas_ref[...]
         panels_v[own, 4] = current
 
-        padded = round_up(leaves, 16)
-
-        def tall(value):
-            extra = jnp.zeros((padded - leaves, value.shape[1]), f32)
-            return jnp.concatenate([value, extra], axis=0).astype(bf16)
-
-        rounded = tall(current)
-        loads[0].wait()
-
-        def unfold(source, scratch, part, count):
-            start = part * group
-            if not isinstance(part, int):
-                start = pl.multiple_of(start, group)
-            block = source[:, pl.ds(start, count), :].astype(f32)
-            width = block.shape[2]
-            for k in range(block.shape[0]):
-                scratch[k * leaf_step : k * leaf_step + count, :width] = block[k]
-
-        def unfolded(scratch, k):
-            return scratch[pl.ds(k, lanes, stride=leaf_step), :].astype(bf16)
-
-        def per_leaf(values, source, scratch, dims, running):
-            def one_group(part, running):
-                unfold(source, scratch, part, group)
-                for k in range(group):
-                    product = lax.dot_general(
-                        values, unfolded(scratch, k), dims, preferred_element_type=f32
-                    )
-                    row = lax.broadcasted_iota(jnp.int32, product.shape, 0)
-                    running = jnp.where(row == part * group + k, product, running)
-                return running
-
-            return lax.fori_loop(0, leaves // group, one_group, running)
-
-        blank = jnp.zeros((padded, lanes), f32)
-        multipoles = per_leaf(rounded, p2m_v, p2m_f, NT, blank)
-        poles_v[own] = jnp.zeros((leaves, lanes), f32)
-        poles_v[own, :, :terms] = multipoles[:leaves, :terms]
+        pattern = (lax.broadcasted_iota(jnp.int32, (window, rows, panels), 1) == 6).astype(f32)
+        right_v[:, :rows, :] = pattern
+        for scratch in (l2p_f, m2l_f):
+            scratch[...] = jnp.zeros(scratch.shape, f32)
+
 
         pl.semaphore_wait(barrier, len(everyone))
 
@@ -166,7 +133,7 @@
 
         def panel_sends():
             buffers = (panels_v, panel_send, panel_recv)
-            for k in range(1, nx):
+            for k in (nx // 2, 1, nx - 1):
                 sent.append(send(*buffers, k - 1, own, own, row_own[k]))
             sent.append(send(*buffers, nx - 1, own, slot_partner + x, partner))
             sent.append(send(*buffers, nx, own, slot_across + x, across))
@@ -190,13 +157,48 @@
 
         pole_set = (poles_v, pole_send, pole_recv)
         panel_set = (panels_v, panel_send, panel_recv)
+        panel_sends()
+
+        padded = round_up(leaves, 16)
+
+        def tall(value):
+            extra = jnp.zeros((padded - leaves, value.shape[1]), f32)
+            return jnp.concatenate([value, extra], axis=0).astype(bf16)
+
+        rounded = tall(current)
+        loads[0].wait()
+
+        def unfold(source, scratch, part, count):
+            start = part * group
+            if not isinstance(part, int):
+                start = pl.multiple_of(start, group)
+            block = source[:, pl.ds(start, count), :].astype(f32)
+            width = block.shape[2]
+            for k in range(block.shape[0]):
+                scratch[k * leaf_step : k * leaf_step + count, :width] = block[k]
+
+        def unfolded(scratch, k):
+            return scratch[pl.ds(k, lanes, stride=leaf_step), :].astype(bf16)
+
+        def per_leaf(values, source, scratch, dims, running):
+            def one_group(part, running):
+                unfold(source, scratch, part, group)
+                for k in range(group):
+                    product = lax.dot_general(
+                        values, unfolded(scratch, k), dims, preferred_element_type=f32
+                    )
+                    row = lax.broadcasted_iota(jnp.int32, product.shape, 0)
+                    running = jnp.where(row == part * group + k, product, running)
+                return running
+
+            return lax.fori_loop(0, leaves // group, one_group, running)
+
+        blank = jnp.zeros((padded, lanes), f32)
+        multipoles = per_leaf(rounded, p2m_v, p2m_f, NT, blank)
+        poles_v[own] = jnp.zeros((leaves, lanes), f32)
+        poles_v[own, :, :terms] = multipoles[:leaves, :terms]
+
         pole_sends()
-        panel_sends()
-
-        pattern = (lax.broadcasted_iota(jnp.int32, (window, rows, panels), 1) == 6).astype(f32)
-        right_v[:, :rows, :] = pattern
-        for scratch in (l2p_f, m2l_f):
-            scratch[...] = jnp.zeros(scratch.shape, f32)
 
         far_v[...] = jnp.full(far_v.shape, -1, jnp.int32)
         off_v[...] = jnp.full(off_v.shape, -1, jnp.int32)
@@ -262,7 +264,6 @@
         tile = jnp.where(tile_lane == krylov + 2, full_sum(folded(mask)), tile)
 
         forward(1)
-        forward(nx - 1)
         loads[1].wait()
 
         def set_apart(part, buffer, count):
@@ -279,6 +280,7 @@
         whole = offsets // group
         steps = whole // buffers
         lax.fori_loop(0, steps // 2, set_apart_all, 0)
+        forward(nx - 1)
         forward(nx // 2)
         lax.fori_loop(steps // 2, steps, set_apart_all, 0)
         for part in range(steps * buffers, whole):

time: 45.8 us -> 44.8 us (0.978)
  Pallas kernels: 41.8 us -> 40.9 us
    pallas_call x1, Pallas kernels: 41.8 us -> 40.9 us  [on_device(): step(basis, coords.transpose(1, 0, 2), areas, counts, near_list, far_list...]
where the time goes in v7:
time: 44.8 us; the launch traced here: 44.6 us
  Pallas kernels  40.9 us (91%)
  local copies, waits for them, and re-layouts  2.44 us (5%)
  between operations  1.29 us (3%)
    pallas_call x1, Pallas kernels, on_device(): step(basis, coords.transpose(1, 0, 2), areas, counts, near_list, far_list...  40.9 us
    unnamed x1, local copies, waits for them, and re-layouts  1.31 us
    squeeze x1, local copies, waits for them, and re-layouts, on_device(): return (vector, hessenberg[0, :krylov + 1])  1.14 us

profile of v7, /device:TPU:1, one launch (start us, length us, event | category | flops | bytes accessed | tf_op | source)
XLA Modules:
  0.0 44.6 jit_solution(10273517324956270524)
XLA Ops:
  1.3 40.9 %shard_map.113 = (f32[24,128]{1,0:T(8,128)}, f32[1,128]{1,0:T(1,128)}) custom-call(f32[8,24,128]{2,1,0:T(8,128)} %basis_ref.1, f32[3,24,128]{2,1,0:T(8,128)} %bitcast.9, f32[24,128]{1,0:T(8,128)} %areas_ref.1, s32[1]{0:T(128)S(6)} %copy.13.counts_ref, s32[24,27]{1,0:T(8,128)} %near_ref.1, s32[24,189]{1,0:T(8,128)} %far_ref.1, s32[24,189]{1,0:T(8,128)} %off_ref.1, ...), custom_call_target="tpu_custom_call" | custom-call | tf_op jit(solution)/shard_map/pallas_call | solution.py:512
  42.1 1.1 %slice_bitcast_fusion = f32[9]{0:T(128)} fusion(f32[1,128]{1,0:T(1,128)} %get-tuple-element.5), kind=kLoop, calls=%fused_computation | loop fusion | bytes 72 | tf_op jit(solution)/shard_map/squeeze | solution.py:516
  43.3 1.3 %copy.14 = f32[24,128]{1,0:T(8,128)} copy(f32[24,128]{1,0:T(8,128)} %get-tuple-element.8) | data formatting | bytes 24576

commit v8 on v7

--- a/solution.py
+++ b/solution.py
@@ -50,7 +50,7 @@
     group = 8
     leaf_step = group + 1
     folded_rows = round_up((lanes - 1) * leaf_step + group, 8)
-    buffers = 4
+    buffers = 8
 
     def kernel(
         basis_ref, coords_ref, areas_ref, counts_ref, near_ref, far_ref, off_ref,
@@ -181,17 +181,16 @@
             return scratch[pl.ds(k, lanes, stride=leaf_step), :].astype(bf16)
 
         def per_leaf(values, source, scratch, dims, running):
-            def one_group(part, running):
-                unfold(source, scratch, part, group)
+            for part in range(leaves // group):
+                unfold(source, scratch.at[part], part, group)
+            for part in range(leaves // group):
                 for k in range(group):
                     product = lax.dot_general(
-                        values, unfolded(scratch, k), dims, preferred_element_type=f32
+                        values, unfolded(scratch.at[part], k), dims, preferred_element_type=f32
                     )
                     row = lax.broadcasted_iota(jnp.int32, product.shape, 0)
                     running = jnp.where(row == part * group + k, product, running)
-                return running
-
-            return lax.fori_loop(0, leaves // group, one_group, running)
+            return running
 
         blank = jnp.zeros((padded, lanes), f32)
         multipoles = per_leaf(rounded, p2m_v, p2m_f, NT, blank)
@@ -219,7 +218,7 @@
             count_v[t] = pairs.astype(bf16)
             return carry
 
-        lax.fori_loop(0, leaves, to_counts, 0, unroll=4)
+        lax.fori_loop(0, leaves, to_counts, 0, unroll=6)
 
         left_v[...] = jnp.zeros(left_v.shape, bf16)
         own_comps = [panels_v[own, comp] - 2.0 for comp in range(3)]
@@ -318,7 +317,7 @@
             sum_v[pl.ds(t * off_step, off_pad), :] = both[:, :lanes] + both[:, lanes:]
             return carry
 
-        lax.fori_loop(0, leaves, to_sums, 0, unroll=6)
+        lax.fori_loop(0, leaves, to_sums, 0, unroll=12)
 
         def to_local(first, count):
             lefts, rights = [], []
@@ -382,7 +381,7 @@
             near_v[...] = jnp.where(pair_lane == t, total, near_v[...])
             return carry
 
-        lax.fori_loop(0, leaves, to_near, 0, unroll=8)
+        lax.fori_loop(0, leaves, to_near, 0, unroll=12)
         nearby = near_v[...].T[:leaves]
 
         image = (0.5 * current + nearby + distant) * mask
@@ -477,8 +476,8 @@
             pltpu.VMEM((window, row_step, panels), f32),
             pltpu.VMEM((leaves * part_step, panels), f32),
             pltpu.VMEM((panels, lanes), f32),
-            pltpu.VMEM((folded_rows, lanes), f32),
-            pltpu.VMEM((folded_rows, lanes), f32),
+            pltpu.VMEM((leaves // group, folded_rows, lanes), f32),
+            pltpu.VMEM((leaves // group, folded_rows, lanes), f32),
             pltpu.VMEM((buffers, folded_rows, lanes), f32),
             pltpu.VMEM((offsets, lanes, lanes), bf16),
             pltpu.VMEM((group_a, krylov, lanes), f32),

time: 44.8 us -> 43.5 us (0.971)
  Pallas kernels: 40.9 us -> 39.6 us
    pallas_call x1, Pallas kernels: 40.9 us -> 39.6 us  [on_device(): step(basis, coords.transpose(1, 0, 2), areas, counts, near_list, far_list...]
where the time goes in v8:
time: 43.5 us; the launch traced here: 43.3 us
  Pallas kernels  39.6 us (91%)
  local copies, waits for them, and re-layouts  2.44 us (6%)
  between operations  1.29 us (3%)
    pallas_call x1, Pallas kernels, on_device(): step(basis, coords.transpose(1, 0, 2), areas, counts, near_list, far_list...  39.6 us
    unnamed x1, local copies, waits for them, and re-layouts  1.31 us
    squeeze x1, local copies, waits for them, and re-layouts, on_device(): return (vector, hessenberg[0, :krylov + 1])  1.14 us

profile of v8, /device:TPU:1, one launch (start us, length us, event | category | flops | bytes accessed | tf_op | source)
XLA Modules:
  0.0 43.3 jit_solution(5533547512205773209)
XLA Ops:
  1.3 39.6 %shard_map.113 = (f32[24,128]{1,0:T(8,128)}, f32[1,128]{1,0:T(1,128)}) custom-call(f32[8,24,128]{2,1,0:T(8,128)} %basis_ref.1, f32[3,24,128]{2,1,0:T(8,128)} %bitcast.9, f32[24,128]{1,0:T(8,128)} %areas_ref.1, s32[1]{0:T(128)S(6)} %copy.13.counts_ref, s32[24,27]{1,0:T(8,128)} %near_ref.1, s32[24,189]{1,0:T(8,128)} %far_ref.1, s32[24,189]{1,0:T(8,128)} %off_ref.1, ...), custom_call_target="tpu_custom_call" | custom-call | tf_op jit(solution)/shard_map/pallas_call | solution.py:511
  40.9 1.1 %slice_bitcast_fusion = f32[9]{0:T(128)} fusion(f32[1,128]{1,0:T(1,128)} %get-tuple-element.5), kind=kLoop, calls=%fused_computation | loop fusion | bytes 72 | tf_op jit(solution)/shard_map/squeeze | solution.py:515
  42.0 1.3 %copy.14 = f32[24,128]{1,0:T(8,128)} copy(f32[24,128]{1,0:T(8,128)} %get-tuple-element.8) | data formatting | bytes 24576

commit v9 on v8

--- a/solution.py
+++ b/solution.py
@@ -152,8 +152,8 @@
             buffers = (panels_v, panel_send, panel_recv)
             received(*buffers, nx + xs[r])
             base = nx + 1 + 2 * (r - 1)
+            sent.append(send(*buffers, base + 1, nx + xs[r], slot_across + xs[r], across))
             sent.append(send(*buffers, base, nx + xs[r], slot_partner + xs[r], partner))
-            sent.append(send(*buffers, base + 1, nx + xs[r], slot_across + xs[r], across))
 
         pole_set = (poles_v, pole_send, pole_recv)
         panel_set = (panels_v, panel_send, panel_recv)
@@ -263,85 +263,10 @@
         tile = jnp.where(tile_lane == krylov + 2, full_sum(folded(mask)), tile)
 
         forward(1)
-        loads[1].wait()
-
-        def set_apart(part, buffer, count):
-            scratch = m2l_f.at[buffer]
-            unfold(m2l_v, scratch, part, count)
-            for k in range(count):
-                pair_v[part * group + k] = unfolded(scratch, k).T
-
-        def set_apart_all(step, carry):
-            for buffer in range(buffers):
-                set_apart(buffers * step + buffer, buffer, group)
-            return carry
-
-        whole = offsets // group
-        steps = whole // buffers
-        lax.fori_loop(0, steps // 2, set_apart_all, 0)
-        forward(nx - 1)
-        forward(nx // 2)
-        lax.fori_loop(steps // 2, steps, set_apart_all, 0)
-        for part in range(steps * buffers, whole):
-            set_apart(part, part % buffers, group)
-        if offsets % group:
-            set_apart(whole, whole % buffers, offsets % group)
-
         valid_before = (seg > 0).astype(f32)
         valid_after = (seg < segments - 1).astype(f32)
 
-        def outside_slots(recv):
-            for k in range(nx):
-                recv(k)
-                recv(2 * nx + k)
-
-        for r in range(1, nx):
-            received(*pole_set, nx + xs[r])
-        outside_slots(lambda slot: received(*pole_set, slot))
-
-        pole_parts = []
-        for slot in range(3 * nx):
-            value = poles_v[slot]
-            if slot < nx:
-                value = value * valid_before
-            if slot >= 2 * nx:
-                value = value * valid_after
-            pole_parts.append(value)
-        pole_parts.append(jnp.zeros((wide - window, lanes), f32))
-        all_poles = jnp.concatenate(pole_parts, axis=0)
-        pole_high, pole_low = high_low(all_poles)
-        both_poles = jnp.concatenate([pole_high, pole_low], axis=1).astype(bf16)
-
-        def to_sums(t, carry):
-            both = jnp.dot(count_v[t], both_poles, preferred_element_type=f32)
-            sum_v[pl.ds(t * off_step, off_pad), :] = both[:, :lanes] + both[:, lanes:]
-            return carry
-
-        lax.fori_loop(0, leaves, to_sums, 0, unroll=12)
-
-        def to_local(first, count):
-            lefts, rights = [], []
-            for o in range(first, first + count):
-                high, low = high_low(sum_v[pl.ds(o, leaves, stride=off_step), :])
-                lefts.append(jnp.concatenate([high, low], axis=0).astype(bf16))
-                rights.append(pair_v[o])
-            return lax.dot_general(
-                jnp.concatenate(lefts, axis=1),
-                jnp.concatenate(rights, axis=0),
-                NN,
-                preferred_element_type=f32,
-            )
-
-        half = round_up(offsets // 2, 2)
-        both = to_local(0, half) + to_local(half, offsets - half)
-        inside = lax.broadcasted_iota(jnp.int32, (leaves, lanes), 1) < terms
-        local = tall(jnp.where(inside, both[:leaves] + both[leaves:], 0.0))
-        loads[2].wait()
-        distant = per_leaf(local, l2p_v, l2p_f, NN, blank)[:leaves]
-
-        outside_slots(lambda slot: received(*panel_set, slot))
-
-        for slot in range(3 * nx):
+        def to_right(slot):
             parts = [two_parts(panels_v[slot, comp] - 2.0) for comp in range(3)]
             area = panels_v[slot, 3]
             weight = area * panels_v[slot, 4] * (1.0 / four_pi)
@@ -358,6 +283,86 @@
             flat = right_v.reshape(window * row_step, panels)
             for k, line in lines:
                 flat[pl.ds(slot * leaves * row_step + k, leaves, stride=row_step), :] = line
+
+        loads[1].wait()
+
+        def set_apart(part, buffer, count):
+            scratch = m2l_f.at[buffer]
+            unfold(m2l_v, scratch, part, count)
+            for k in range(count):
+                pair_v[part * group + k] = unfolded(scratch, k).T
+
+        def set_apart_all(step, carry):
+            for buffer in range(buffers):
+                set_apart(buffers * step + buffer, buffer, group)
+            return carry
+
+        whole = offsets // group
+        steps = whole // buffers
+        lax.fori_loop(0, steps // 2, set_apart_all, 0)
+        forward(nx - 1)
+        forward(nx // 2)
+        for slot in range(nx, 2 * nx):
+            to_right(slot)
+        lax.fori_loop(steps // 2, steps, set_apart_all, 0)
+        for part in range(steps * buffers, whole):
+            set_apart(part, part % buffers, group)
+        if offsets % group:
+            set_apart(whole, whole % buffers, offsets % group)
+
+        def outside_slots(recv):
+            for k in range(nx):
+                recv(k)
+                recv(2 * nx + k)
+
+        for r in range(1, nx):
+            received(*pole_set, nx + xs[r])
+        outside_slots(lambda slot: received(*pole_set, slot))
+
+        pole_parts = []
+        for slot in range(3 * nx):
+            value = poles_v[slot]
+            if slot < nx:
+                value = value * valid_before
+            if slot >= 2 * nx:
+                value = value * valid_after
+            pole_parts.append(value)
+        pole_parts.append(jnp.zeros((wide - window, lanes), f32))
+        all_poles = jnp.concatenate(pole_parts, axis=0)
+        pole_high, pole_low = high_low(all_poles)
+        both_poles = jnp.concatenate([pole_high, pole_low], axis=1).astype(bf16)
+
+        def to_sums(t, carry):
+            both = jnp.dot(count_v[t], both_poles, preferred_element_type=f32)
+            sum_v[pl.ds(t * off_step, off_pad), :] = both[:, :lanes] + both[:, lanes:]
+            return carry
+
+        lax.fori_loop(0, leaves, to_sums, 0, unroll=12)
+
+        def to_local(first, count):
+            lefts, rights = [], []
+            for o in range(first, first + count):
+                high, low = high_low(sum_v[pl.ds(o, leaves, stride=off_step), :])
+                lefts.append(jnp.concatenate([high, low], axis=0).astype(bf16))
+                rights.append(pair_v[o])
+            return lax.dot_general(
+                jnp.concatenate(lefts, axis=1),
+                jnp.concatenate(rights, axis=0),
+                NN,
+                preferred_element_type=f32,
+            )
+
+        half = round_up(offsets // 2, 2)
+        both = to_local(0, half) + to_local(half, offsets - half)
+        inside = lax.broadcasted_iota(jnp.int32, (leaves, lanes), 1) < terms
+        local = tall(jnp.where(inside, both[:leaves] + both[leaves:], 0.0))
+        loads[2].wait()
+        distant = per_leaf(local, l2p_v, l2p_f, NN, blank)[:leaves]
+
+        outside_slots(lambda slot: received(*panel_set, slot))
+
+        for slot in [*range(nx), *range(2 * nx, 3 * nx)]:
+            to_right(slot)
 
         near_v[...] = jnp.zeros(near_v.shape, f32)
         pair_lane = lax.broadcasted_iota(jnp.int32, (panels, lanes), 1)

time: 43.5 us -> 43.5 us (level)
  no operation moved by 1% of the time
where the time goes in v9:
time: 43.5 us; the launch traced here: 43.3 us
  Pallas kernels  39.6 us (91%)
  local copies, waits for them, and re-layouts  2.44 us (6%)
  between operations  1.29 us (3%)
    pallas_call x1, Pallas kernels, on_device(): step(basis, coords.transpose(1, 0, 2), areas, counts, near_list, far_list...  39.6 us
    unnamed x1, local copies, waits for them, and re-layouts  1.31 us
    squeeze x1, local copies, waits for them, and re-layouts, on_device(): return (vector, hessenberg[0, :krylov + 1])  1.14 us

profile of v9, /device:TPU:1, one launch (start us, length us, event | category | flops | bytes accessed | tf_op | source)
XLA Modules:
  0.0 43.3 jit_solution(13901202103187950867)
XLA Ops:
  1.3 39.6 %shard_map.113 = (f32[24,128]{1,0:T(8,128)}, f32[1,128]{1,0:T(1,128)}) custom-call(f32[8,24,128]{2,1,0:T(8,128)} %basis_ref.1, f32[3,24,128]{2,1,0:T(8,128)} %bitcast.9, f32[24,128]{1,0:T(8,128)} %areas_ref.1, s32[1]{0:T(128)S(6)} %copy.13.counts_ref, s32[24,27]{1,0:T(8,128)} %near_ref.1, s32[24,189]{1,0:T(8,128)} %far_ref.1, s32[24,189]{1,0:T(8,128)} %off_ref.1, ...), custom_call_target="tpu_custom_call" | custom-call | tf_op jit(solution)/shard_map/pallas_call | solution.py:516
  40.9 1.1 %slice_bitcast_fusion = f32[9]{0:T(128)} fusion(f32[1,128]{1,0:T(1,128)} %get-tuple-element.5), kind=kLoop, calls=%fused_computation | loop fusion | bytes 72 | tf_op jit(solution)/shard_map/squeeze | solution.py:520
  42.0 1.3 %copy.14 = f32[24,128]{1,0:T(8,128)} copy(f32[24,128]{1,0:T(8,128)} %get-tuple-element.8) | data formatting | bytes 24576
